TPU v7x, 32 devices: a whole 2x2x4 slice. The times are simulated.
32 devices in a mesh: dp: 2 (over x), sx: 4 (over z), sy: 4 (over y, core).
Axes of the slice: x: 2, y: 2, z: 4, core: 2. Of those that a mesh axis runs over, the one named last changes fastest.
Arguments:
- act_in: bfloat16 [24, 1024, 32, 256], P('dp', 'sy', 'sx'), parts along dimension 0
- norm_first: bfloat16 [2, 256], replicated
- w_first: bfloat16 [3, 3, 256, 128], replicated
- w_short: bfloat16 [256, 128], replicated
- norm_rest: bfloat16 [6, 2, 128], replicated
- w_rest: bfloat16 [5, 3, 3, 128, 128], replicated
- bias_rest: bfloat16 [7, 128], replicated
- w_out: bfloat16 [3, 3, 128, 3], replicated
- bias_out: bfloat16 [3], replicated
Outputs:
- output: float32 [24, 1024, 32, 3], P('dp', 'sy', 'sx'), parts along dimension 0
There are 2 independent parts. A program takes and returns all parts, laid end to end along the dimension named above; an argument that names none is the same for every part.
All inputs are finite; a program needn't handle non-finite values.
Results may differ from a plain program's by a relative error of at most 0.00909453.
Values are sent between devices in bfloat16 or wider.
A program may use at most 1 GiB of HBM per device.

v0:
```python
import jax
import jax.numpy as jnp
from jax import lax
from jax.sharding import PartitionSpec as P

GROUPS = 32
GN_EPS = 1e-6


def solution(mesh):
    rows_n = mesh.shape["sy"]
    cols_n = mesh.shape["sx"]
    to_below = [(position, position + 1) for position in range(rows_n - 1)]
    to_above = [(position + 1, position) for position in range(rows_n - 1)]
    to_right = [(position, position + 1) for position in range(cols_n - 1)]
    to_left = [(position + 1, position) for position in range(cols_n - 1)]
    tile_spec = P("dp", "sy", "sx", None)
    replicated = P()

    def add_border(act_map):
        top_row = lax.ppermute(act_map[:, -1:], "sy", to_below)
        bottom_row = lax.ppermute(act_map[:, :1], "sy", to_above)
        tall = jnp.concatenate([top_row, act_map, bottom_row], axis=1)
        left_col = lax.ppermute(tall[:, :, -1:], "sx", to_right)
        right_col = lax.ppermute(tall[:, :, :1], "sx", to_left)
        return jnp.concatenate([left_col, tall, right_col], axis=2)

    def conv_tile(act_map, kernel):
        return lax.conv_general_dilated(add_border(act_map), kernel, (1, 1), ((0, 0), (0, 0)), dimension_numbers=("NHWC", "HWIO", "NHWC"), preferred_element_type=jnp.float32)

    def group_norm_act(act_map, norm_pair):
        samples = act_map.shape[0]
        per_group = act_map.shape[3] // GROUPS
        group_count = act_map.shape[1] * rows_n * act_map.shape[2] * cols_n * per_group
        sum_one = jnp.sum(act_map, axis=(1, 2), dtype=jnp.float32).reshape(samples, GROUPS, per_group).sum(axis=2)
        sum_two = jnp.sum(jnp.square(act_map.astype(jnp.float32)), axis=(1, 2)).reshape(samples, GROUPS, per_group).sum(axis=2)
        totals = lax.psum(jnp.stack([sum_one, sum_two], axis=-1), ("sy", "sx"))
        group_mean = totals[:, :, 0] / group_count
        inv_std = lax.rsqrt(totals[:, :, 1] / group_count - group_mean * group_mean + GN_EPS)
        chan_scale = jnp.repeat(inv_std, per_group, axis=1) * norm_pair[0].astype(jnp.float32)
        chan_shift = norm_pair[1].astype(jnp.float32) - jnp.repeat(group_mean, per_group, axis=1) * chan_scale
        return jax.nn.silu(act_map.astype(jnp.float32) * chan_scale[:, None, None, :] + chan_shift[:, None, None, :]).astype(jnp.bfloat16)

    def local_decode(act_in, norm_first, w_first, w_short, norm_rest, w_rest, bias_rest, w_out, bias_out):
        bias_rows = bias_rest.astype(jnp.float32)
        mid_act = (conv_tile(group_norm_act(act_in, norm_first), w_first) + bias_rows[0]).astype(jnp.bfloat16)
        skip_path = jnp.einsum("nhwc,cd->nhwd", act_in, w_short, preferred_element_type=jnp.float32) + bias_rows[6]
        hidden = (conv_tile(group_norm_act(mid_act, norm_rest[0]), w_rest[0]) + bias_rows[1] + skip_path).astype(jnp.bfloat16)
        for res_index in range(1, 3):
            first_at = 2 * res_index - 1
            mid_act = (conv_tile(group_norm_act(hidden, norm_rest[first_at]), w_rest[first_at]) + bias_rows[first_at + 1]).astype(jnp.bfloat16)
            hidden = (conv_tile(group_norm_act(mid_act, norm_rest[first_at + 1]), w_rest[first_at + 1]) + bias_rows[first_at + 2] + hidden.astype(jnp.float32)).astype(jnp.bfloat16)
        return conv_tile(group_norm_act(hidden, norm_rest[5]), w_out) + bias_out.astype(jnp.float32)

    return jax.shard_map(local_decode, mesh=mesh, in_specs=(tile_spec, replicated, replicated, replicated, replicated, replicated, replicated, replicated, replicated), out_specs=tile_spec, check_vma=False)
```

profile of v0, /device:TPU:0, one launch (start us, length us, event | category | flops | bytes accessed | tf_op | source)
XLA Modules:
  0.0 1002.9 jit_solution(7395595096043242738)
XLA Ops:
  0.0 19.7 %convert_reduce_fusion = (f32[12,256]{1,0:T(8,128)S(1)}, f32[12,256]{1,0:T(8,128)S(1)}) fusion(bf16[12,256,8,256]{3,2,1,0:T(8,128)(2,1)} %param.9), kind=kLoop, calls=%fused_computation.2 | loop fusion | flops 25159680 | bytes 12607488 | tf_op jit(solution)/shard_map/reduce_sum | solution.py:35
  20.3 63.4 %psum.49 = f32[12,32,2]{1,0,2:T(8,128)S(1)} all-reduce(f32[12,32,2]{1,0,2:T(8,128)S(1)} %pad_maximum_fusion.21), channel_id=1, replica_groups=mesh['dp'=2,'sx'=4,'sy'=4] {'sy','sx'}, use_global_device_ids=true, to_apply=%region_4.0 | all-reduce | flops 768 | bytes 6144 | tf_op jit(solution)/shard_map/psum | solution.py:37
  84.2 24.2 %fusion.7 = bf16[12,256,8,256]{3,0,2,1:T(8,128)(2,1)S(1)} fusion(bf16[12,256,8,256]{3,2,1,0:T(8,128)(2,1)} %param.9, f32[12,256]{1,0:T(8,128)S(1)} %get-tuple-element.31, f32[12,256]{1,0:T(8,128)S(1)} %get-tuple-element.32), kind=kLoop, calls=%fused_computation.10 | loop fusion | flops 50331648 | bytes 25190400 | tf_op jit(solution)/shard_map/convert_element_type | solution.py:42
  119.9 30.2 %collective-permute-done.2 = bf16[12,258,1,256]{3,1,2,0:T(8,128)(2,1)S(1)} collective-permute-done((bf16[12,258,1,256]{3,1,2,0:T(8,128)(2,1)S(1)}, bf16[12,258,1,256]{3,1,2,0:T(8,128)(2,1)S(1)}, u32[]{:S(2)}, u32[]{:S(2)}) %collective-permute-start.2) | collective-permute-done | bytes 1585184 | tf_op jit(solution)/shard_map/ppermute | solution.py:24
  155.8 43.5 %convert_reduce_fusion.6 = (f32[12,128]{1,0:T(8,128)S(1)}, f32[12,128]{1,0:T(8,128)S(1)}, bf16[12,256,8,128]{3,0,2,1:T(8,128)(2,1)}) fusion(f32[128]{0:T(128)S(1)} %get-tuple-element.67, bf16[3,3,256,128]{3,2,1,0:T(8,128)(2,1)S(1)} %copy-done, bf16[12,258,1,256]{3,0,2,1:T(8,128)(2,1)S(1)} %copy.345, bf16[12,1,8,256]{3,0,2,1:T(8,128)(2,1)S(1)} %collective-permute-done.1, ...), kind=kOutput, calls=%fused_computation.30 | convolution fusion | flops 14546087936 | bytes 22745600 | tf_op jit(solution)/shard_map/conv_general_dilated | solution.py:29
  199.8 58.8 %psum.50 = f32[12,32,2]{1,0,2:T(8,128)S(1)} all-reduce(f32[12,32,2]{1,0,2:T(8,128)S(1)} %pad_maximum_fusion.22), channel_id=1, replica_groups=mesh['dp'=2,'sx'=4,'sy'=4] {'sy','sx'}, use_global_device_ids=true, to_apply=%region_9.10 | all-reduce | flops 768 | bytes 6144 | tf_op jit(solution)/shard_map/psum | solution.py:37
  258.9 7.0 fusion.25
  276.4 12.6 %fusion.154 = f32[12,256,8,128]{3,2,1,0:T(8,128)} fusion(bf16[12,256,8,256]{3,2,1,0:T(8,128)(2,1)} %param.9, bf16[256,128]{1,0:T(8,128)(2,1)S(1)} %copy-done.3), kind=kOutput, calls=%fused_computation.189 | convolution fusion | flops 1610612736 | bytes 25231360 | tf_op jit(solution)/shard_map/nhwc,cd->nhwd/dot_general | solution.py:47
  296.4 31.8 %convert_reduce_fusion.2 = (f32[12,128]{1,0:T(8,128)S(1)}, f32[12,128]{1,0:T(8,128)S(1)}, bf16[12,256,8,128]{3,0,2,1:T(8,128)(2,1)}) fusion(f32[128]{0:T(128)S(1)} %get-tuple-element.65, f32[12,256,8,128]{3,2,1,0:T(8,128)} %fusion.154, f32[128]{0:T(128)S(1)} %get-tuple-element.66, bf16[5,3,3,128,128]{4,3,2,1,0:T(8,128)(2,1)S(1)} %copy-done.18, ...), kind=kOutput, calls=%fused_computation.18 | convolution fusion | flops 7288771584 | bytes 27653120 | tf_op jit(solution)/shard_map/conv_general_dilated | solution.py:29
  328.7 58.4 %psum.51 = f32[12,32,2]{1,0,2:T(8,128)S(1)} all-reduce(f32[12,32,2]{1,0,2:T(8,128)S(1)} %pad_maximum_fusion.23), channel_id=1, replica_groups=mesh['dp'=2,'sx'=4,'sy'=4] {'sy','sx'}, use_global_device_ids=true, to_apply=%region_14.15 | all-reduce | flops 768 | bytes 6144 | tf_op jit(solution)/shard_map/psum | solution.py:37
  404.0 15.2 %collective-permute-done.10 = bf16[12,258,1,128]{3,1,2,0:T(8,128)(2,1)S(1)} collective-permute-done((bf16[12,258,1,128]{3,1,2,0:T(8,128)(2,1)S(1)}, bf16[12,258,1,128]{3,1,2,0:T(8,128)(2,1)S(1)}, u32[]{:S(2)}, u32[]{:S(2)}) %collective-permute-start.10) | collective-permute-done | bytes 792608 | tf_op jit(solution)/shard_map/ppermute | solution.py:24
  424.4 21.9 %convert_reduce_fusion.5 = (f32[12,128]{1,0:T(8,128)S(1)}, f32[12,128]{1,0:T(8,128)S(1)}, bf16[12,256,8,128]{3,0,2,1:T(8,128)(2,1)}) fusion(f32[128]{0:T(128)S(1)} %get-tuple-element.64, bf16[5,3,3,128,128]{4,3,2,1,0:T(8,128)(2,1)S(1)} %copy-done.18, bf16[12,258,1,128]{3,0,2,1:T(8,128)(2,1)S(1)} %copy.371, ...), kind=kOutput, calls=%fused_computation.27 | convolution fusion | flops 7282480128 | bytes 17166848 | tf_op jit(solution)/shard_map/conv_general_dilated | solution.py:29
  446.8 58.2 %psum.52 = f32[12,32,2]{1,0,2:T(8,128)S(1)} all-reduce(f32[12,32,2]{1,0,2:T(8,128)S(1)} %pad_maximum_fusion.24), channel_id=1, replica_groups=mesh['dp'=2,'sx'=4,'sy'=4] {'sy','sx'}, use_global_device_ids=true, to_apply=%region_19.20 | all-reduce | flops 768 | bytes 6144 | tf_op jit(solution)/shard_map/psum | solution.py:37
  522.7 15.0 %collective-permute-done.14 = bf16[12,258,1,128]{3,1,2,0:T(8,128)(2,1)S(1)} collective-permute-done((bf16[12,258,1,128]{3,1,2,0:T(8,128)(2,1)S(1)}, bf16[12,258,1,128]{3,1,2,0:T(8,128)(2,1)S(1)}, u32[]{:S(2)}, u32[]{:S(2)}) %collective-permute-start.14) | collective-permute-done | bytes 792608 | tf_op jit(solution)/shard_map/ppermute | solution.py:24
  542.8 23.2 %convert_reduce_fusion.1 = (f32[12,128]{1,0:T(8,128)S(1)}, f32[12,128]{1,0:T(8,128)S(1)}, bf16[12,256,8,128]{3,0,2,1:T(8,128)(2,1)}) fusion(bf16[12,256,8,128]{3,0,2,1:T(8,128)(2,1)S(1)} %bitcast.208, f32[128]{0:T(128)S(1)} %copy-done.17, bf16[5,3,3,128,128]{4,3,2,1,0:T(8,128)(2,1)S(1)} %copy-done.18, bf16[12,258,1,128]{3,0,2,1:T(8,128)(2,1)S(1)} %copy.383, ...), kind=kOutput, calls=%fused_computation.14 | convolution fusion | flops 7288771584 | bytes 25555456 | tf_op jit(solution)/shard_map/conv_general_dilated | solution.py:29
  566.5 58.2 %psum.53 = f32[12,32,2]{1,0,2:T(8,128)S(1)} all-reduce(f32[12,32,2]{1,0,2:T(8,128)S(1)} %pad_maximum_fusion.25), channel_id=1, replica_groups=mesh['dp'=2,'sx'=4,'sy'=4] {'sy','sx'}, use_global_device_ids=true, to_apply=%region_24.25 | all-reduce | flops 768 | bytes 6144 | tf_op jit(solution)/shard_map/psum | solution.py:37
  642.0 14.8 %collective-permute-done.18 = bf16[12,258,1,128]{3,1,2,0:T(8,128)(2,1)S(1)} collective-permute-done((bf16[12,258,1,128]{3,1,2,0:T(8,128)(2,1)S(1)}, bf16[12,258,1,128]{3,1,2,0:T(8,128)(2,1)S(1)}, u32[]{:S(2)}, u32[]{:S(2)}) %collective-permute-start.18) | collective-permute-done | bytes 792608 | tf_op jit(solution)/shard_map/ppermute | solution.py:24
  662.0 21.9 %convert_reduce_fusion.4 = (f32[12,128]{1,0:T(8,128)S(1)}, f32[12,128]{1,0:T(8,128)S(1)}, bf16[12,256,8,128]{3,0,2,1:T(8,128)(2,1)}) fusion(f32[128]{0:T(128)S(1)} %copy-done.16, bf16[5,3,3,128,128]{4,3,2,1,0:T(8,128)(2,1)S(1)} %copy-done.18, bf16[12,258,1,128]{3,0,2,1:T(8,128)(2,1)S(1)} %copy.395, bf16[12,1,8,128]{3,0,2,1:T(8,128)(2,1)S(1)} %collective-permute-done.17, ...), kind=kOutput, calls=%fused_computation.24 | convolution fusion | flops 7282480128 | bytes 17166848 | tf_op jit(solution)/shard_map/conv_general_dilated | solution.py:29
  684.4 58.1 %psum.54 = f32[12,32,2]{1,0,2:T(8,128)S(1)} all-reduce(f32[12,32,2]{1,0,2:T(8,128)S(1)} %pad_maximum_fusion.26), channel_id=1, replica_groups=mesh['dp'=2,'sx'=4,'sy'=4] {'sy','sx'}, use_global_device_ids=true, to_apply=%region_29.30 | all-reduce | flops 768 | bytes 6144 | tf_op jit(solution)/shard_map/psum | solution.py:37
  760.2 15.0 %collective-permute-done.22 = bf16[12,258,1,128]{3,1,2,0:T(8,128)(2,1)S(1)} collective-permute-done((bf16[12,258,1,128]{3,1,2,0:T(8,128)(2,1)S(1)}, bf16[12,258,1,128]{3,1,2,0:T(8,128)(2,1)S(1)}, u32[]{:S(2)}, u32[]{:S(2)}) %collective-permute-start.22) | collective-permute-done | bytes 792608 | tf_op jit(solution)/shard_map/ppermute | solution.py:24
  780.4 23.2 %convert_reduce_fusion.3 = (f32[12,128]{1,0:T(8,128)S(1)}, f32[12,128]{1,0:T(8,128)S(1)}, bf16[12,256,8,128]{3,0,2,1:T(8,128)(2,1)}) fusion(bf16[12,256,8,128]{3,0,2,1:T(8,128)(2,1)S(1)} %bitcast.210, f32[128]{0:T(128)S(1)} %copy-done.15, bf16[5,3,3,128,128]{4,3,2,1,0:T(8,128)(2,1)S(1)} %copy-done.18, bf16[12,258,1,128]{3,0,2,1:T(8,128)(2,1)S(1)} %copy.407, ...), kind=kOutput, calls=%fused_computation.21 | convolution fusion | flops 7288771584 | bytes 25555456 | tf_op jit(solution)/shard_map/conv_general_dilated | solution.py:29
  804.1 58.2 %psum.55 = f32[12,32,2]{1,0,2:T(8,128)S(1)} all-reduce(f32[12,32,2]{1,0,2:T(8,128)S(1)} %pad_maximum_fusion.27), channel_id=1, replica_groups=mesh['dp'=2,'sx'=4,'sy'=4] {'sy','sx'}, use_global_device_ids=true, to_apply=%region_34.35 | all-reduce | flops 768 | bytes 6144 | tf_op jit(solution)/shard_map/psum | solution.py:37
  879.2 15.2 %collective-permute-done.26 = bf16[12,258,1,128]{3,1,2,0:T(8,128)(2,1)S(1)} collective-permute-done((bf16[12,258,1,128]{3,1,2,0:T(8,128)(2,1)S(1)}, bf16[12,258,1,128]{3,1,2,0:T(8,128)(2,1)S(1)}, u32[]{:S(2)}, u32[]{:S(2)}) %collective-permute-start.26) | collective-permute-done | bytes 792608 | tf_op jit(solution)/shard_map/ppermute | solution.py:24
  899.6 99.1 %broadcast_add_fusion = f32[12,256,8,3]{0,3,2,1:T(4,128)} fusion(f32[3]{0:T(128)S(1)} %convert_element_type.251, bf16[3,3,128,3]{2,3,1,0:T(4,128)(2,1)S(1)} %copy-done.19, bf16[12,258,1,128]{3,0,2,1:T(8,128)(2,1)S(1)} %copy.419, bf16[12,1,8,128]{3,0,2,1:T(8,128)(2,1)S(1)} %collective-permute-done.25, bf16[12,256,8,128]{3,0,2,1:T(8,128)(2,1)S(1)} %fusion.49, ...), kind=kOutput, calls=%fused_computation.160 | convolution fusion | flops 185794560 | bytes 8227596 | tf_op jit(solution)/shard_map/conv_general_dilated | solution.py:29
  (263 shorter events, 154.5 us)
Async XLA Ops:
  109.8 3.9 collective-permute-start.1
  115.2 34.9 %collective-permute-start.2 = (bf16[12,258,1,256]{3,1,2,0:T(8,128)(2,1)S(1)}, bf16[12,258,1,256]{3,1,2,0:T(8,128)(2,1)S(1)}, u32[]{:S(2)}, u32[]{:S(2)}) collective-permute-start(bf16[12,258,1,256]{3,1,2,0:T(8,128)(2,1)S(1)} %copy.342), channel_id=1, source_target_pairs={{0,4},{4,8},{8,12},{1,5},{5,9},{9,13},{2,6},{6,10},{10,14},{3,7},{... | collective-permute-start | bytes 4755464 | tf_op jit(solution)/shard_map/ppermute | solution.py:24
  117.2 38.3 %collective-permute-start.3 = (bf16[12,258,1,256]{3,1,2,0:T(8,128)(2,1)S(1)}, bf16[12,258,1,256]{3,1,2,0:T(8,128)(2,1)S(1)}, u32[]{:S(2)}, u32[]{:S(2)}) collective-permute-start(bf16[12,258,1,256]{3,1,2,0:T(8,128)(2,1)S(1)} %copy.343), channel_id=1, source_target_pairs={{4,0},{8,4},{12,8},{5,1},{9,5},{13,9},{6,2},{10,6},{14,10},{7,3},{... | collective-permute-start | bytes 4755464 | tf_op jit(solution)/shard_map/ppermute | solution.py:25
  265.9 2.7 collective-permute-start.4
  267.4 4.7 collective-permute-start.5
  272.7 18.4 %collective-permute-start.6 = (bf16[12,258,1,128]{3,1,2,0:T(8,128)(2,1)S(1)}, bf16[12,258,1,128]{3,1,2,0:T(8,128)(2,1)S(1)}, u32[]{:S(2)}, u32[]{:S(2)}) collective-permute-start(bf16[12,258,1,128]{3,1,2,0:T(8,128)(2,1)S(1)} %copy.354), channel_id=1, source_target_pairs={{0,4},{4,8},{8,12},{1,5},{5,9},{9,13},{2,6},{6,10},{10,14},{3,7},{... | collective-permute-start | bytes 2377736 | tf_op jit(solution)/shard_map/ppermute | solution.py:24
  274.6 21.6 %collective-permute-start.7 = (bf16[12,258,1,128]{3,1,2,0:T(8,128)(2,1)S(1)}, bf16[12,258,1,128]{3,1,2,0:T(8,128)(2,1)S(1)}, u32[]{:S(2)}, u32[]{:S(2)}) collective-permute-start(bf16[12,258,1,128]{3,1,2,0:T(8,128)(2,1)S(1)} %copy.355), channel_id=1, source_target_pairs={{4,0},{8,4},{12,8},{5,1},{9,5},{13,9},{6,2},{10,6},{14,10},{7,3},{... | collective-permute-start | bytes 2377736 | tf_op jit(solution)/shard_map/ppermute | solution.py:25
  395.8 4.4 collective-permute-start.9
  400.8 18.4 %collective-permute-start.10 = (bf16[12,258,1,128]{3,1,2,0:T(8,128)(2,1)S(1)}, bf16[12,258,1,128]{3,1,2,0:T(8,128)(2,1)S(1)}, u32[]{:S(2)}, u32[]{:S(2)}) collective-permute-start(bf16[12,258,1,128]{3,1,2,0:T(8,128)(2,1)S(1)} %copy.368), channel_id=1, source_target_pairs={{0,4},{4,8},{8,12},{1,5},{5,9},{9,13},{2,6},{6,10},{10,14},{3,7},{... | collective-permute-start | bytes 2377736 | tf_op jit(solution)/shard_map/ppermute | solution.py:24
  402.7 21.5 %collective-permute-start.11 = (bf16[12,258,1,128]{3,1,2,0:T(8,128)(2,1)S(1)}, bf16[12,258,1,128]{3,1,2,0:T(8,128)(2,1)S(1)}, u32[]{:S(2)}, u32[]{:S(2)}) collective-permute-start(bf16[12,258,1,128]{3,1,2,0:T(8,128)(2,1)S(1)} %copy.369), channel_id=1, source_target_pairs={{4,0},{8,4},{12,8},{5,1},{9,5},{13,9},{6,2},{10,6},{14,10},{7,3},{... | collective-permute-start | bytes 2377736 | tf_op jit(solution)/shard_map/ppermute | solution.py:25
  512.4 3.1 collective-permute-start.12
  514.0 4.6 collective-permute-start.13
  519.2 18.4 %collective-permute-start.14 = (bf16[12,258,1,128]{3,1,2,0:T(8,128)(2,1)S(1)}, bf16[12,258,1,128]{3,1,2,0:T(8,128)(2,1)S(1)}, u32[]{:S(2)}, u32[]{:S(2)}) collective-permute-start(bf16[12,258,1,128]{3,1,2,0:T(8,128)(2,1)S(1)} %copy.380), channel_id=1, source_target_pairs={{0,4},{4,8},{8,12},{1,5},{5,9},{9,13},{2,6},{6,10},{10,14},{3,7},{... | collective-permute-start | bytes 2377736 | tf_op jit(solution)/shard_map/ppermute | solution.py:24
  521.1 21.5 %collective-permute-start.15 = (bf16[12,258,1,128]{3,1,2,0:T(8,128)(2,1)S(1)}, bf16[12,258,1,128]{3,1,2,0:T(8,128)(2,1)S(1)}, u32[]{:S(2)}, u32[]{:S(2)}) collective-permute-start(bf16[12,258,1,128]{3,1,2,0:T(8,128)(2,1)S(1)} %copy.381), channel_id=1, source_target_pairs={{4,0},{8,4},{12,8},{5,1},{9,5},{13,9},{6,2},{10,6},{14,10},{7,3},{... | collective-permute-start | bytes 2377736 | tf_op jit(solution)/shard_map/ppermute | solution.py:25
  633.4 4.4 collective-permute-start.17
  638.4 18.4 %collective-permute-start.18 = (bf16[12,258,1,128]{3,1,2,0:T(8,128)(2,1)S(1)}, bf16[12,258,1,128]{3,1,2,0:T(8,128)(2,1)S(1)}, u32[]{:S(2)}, u32[]{:S(2)}) collective-permute-start(bf16[12,258,1,128]{3,1,2,0:T(8,128)(2,1)S(1)} %copy.392), channel_id=1, source_target_pairs={{0,4},{4,8},{8,12},{1,5},{5,9},{9,13},{2,6},{6,10},{10,14},{3,7},{... | collective-permute-start | bytes 2377736 | tf_op jit(solution)/shard_map/ppermute | solution.py:24
  640.3 21.5 %collective-permute-start.19 = (bf16[12,258,1,128]{3,1,2,0:T(8,128)(2,1)S(1)}, bf16[12,258,1,128]{3,1,2,0:T(8,128)(2,1)S(1)}, u32[]{:S(2)}, u32[]{:S(2)}) collective-permute-start(bf16[12,258,1,128]{3,1,2,0:T(8,128)(2,1)S(1)} %copy.393), channel_id=1, source_target_pairs={{4,0},{8,4},{12,8},{5,1},{9,5},{13,9},{6,2},{10,6},{14,10},{7,3},{... | collective-permute-start | bytes 2377736 | tf_op jit(solution)/shard_map/ppermute | solution.py:25
  750.0 3.1 collective-permute-start.20
  751.5 4.7 collective-permute-start.21
  756.8 18.4 %collective-permute-start.22 = (bf16[12,258,1,128]{3,1,2,0:T(8,128)(2,1)S(1)}, bf16[12,258,1,128]{3,1,2,0:T(8,128)(2,1)S(1)}, u32[]{:S(2)}, u32[]{:S(2)}) collective-permute-start(bf16[12,258,1,128]{3,1,2,0:T(8,128)(2,1)S(1)} %copy.404), channel_id=1, source_target_pairs={{0,4},{4,8},{8,12},{1,5},{5,9},{9,13},{2,6},{6,10},{10,14},{3,7},{... | collective-permute-start | bytes 2377736 | tf_op jit(solution)/shard_map/ppermute | solution.py:24
  758.7 21.5 %collective-permute-start.23 = (bf16[12,258,1,128]{3,1,2,0:T(8,128)(2,1)S(1)}, bf16[12,258,1,128]{3,1,2,0:T(8,128)(2,1)S(1)}, u32[]{:S(2)}, u32[]{:S(2)}) collective-permute-start(bf16[12,258,1,128]{3,1,2,0:T(8,128)(2,1)S(1)} %copy.405), channel_id=1, source_target_pairs={{4,0},{8,4},{12,8},{5,1},{9,5},{13,9},{6,2},{10,6},{14,10},{7,3},{... | collective-permute-start | bytes 2377736 | tf_op jit(solution)/shard_map/ppermute | solution.py:25
  871.0 4.3 collective-permute-start.25
  876.0 18.4 %collective-permute-start.26 = (bf16[12,258,1,128]{3,1,2,0:T(8,128)(2,1)S(1)}, bf16[12,258,1,128]{3,1,2,0:T(8,128)(2,1)S(1)}, u32[]{:S(2)}, u32[]{:S(2)}) collective-permute-start(bf16[12,258,1,128]{3,1,2,0:T(8,128)(2,1)S(1)} %copy.416), channel_id=1, source_target_pairs={{0,4},{4,8},{8,12},{1,5},{5,9},{9,13},{2,6},{6,10},{10,14},{3,7},{... | collective-permute-start | bytes 2377736 | tf_op jit(solution)/shard_map/ppermute | solution.py:24
  877.9 21.5 %collective-permute-start.27 = (bf16[12,258,1,128]{3,1,2,0:T(8,128)(2,1)S(1)}, bf16[12,258,1,128]{3,1,2,0:T(8,128)(2,1)S(1)}, u32[]{:S(2)}, u32[]{:S(2)}) collective-permute-start(bf16[12,258,1,128]{3,1,2,0:T(8,128)(2,1)S(1)} %copy.417), channel_id=1, source_target_pairs={{4,0},{8,4},{12,8},{5,1},{9,5},{13,9},{6,2},{10,6},{14,10},{7,3},{... | collective-permute-start | bytes 2377736 | tf_op jit(solution)/shard_map/ppermute | solution.py:25
  (29 other events, 1311.1 us)
where the time goes:
time: 1010 us; the launch traced here: 1000 us
  blocking collectives  413 us (41%)
  matrix products  277 us (27%)
  waiting for transfers between devices  163 us (16%)
  other arithmetic  91 us (9%)
  starting transfers between devices  41.3 us (4%)
  local copies, waits for them, and re-layouts  16 us (2%)
    psum x7, blocking collectives, group_norm_act(): totals = lax.psum(jnp.stack([sum_one, sum_two], axis=-1), ('sy', 'sx'))  413 us
    conv_general_dilated x7, matrix products, conv_tile(): lax.conv_general_dilated(add_border(act_map), kernel, (1, 1), ((0, 0), (0...  265 us
    ppermute x7, waiting for transfers between devices, add_border(): left_col = lax.ppermute(tall[:, :, -1:], 'sx', to_right)  107 us
    convert_element_type x7, other arithmetic, group_norm_act(): jax.nn.silu(act_map.astype(jnp.float32) * chan_scale[:, None, None, :] +...  66.1 us
    ppermute x7, waiting for transfers between devices, add_border(): right_col = lax.ppermute(tall[:, :, :1], 'sx', to_left)  33.8 us
    ppermute x7, waiting for transfers between devices, add_border(): bottom_row = lax.ppermute(act_map[:, :1], 'sy', to_above)  21.2 us
  transfers between devices with their start and end apart: 28, of which 21 were waited for; matrix products, arithmetic and copies ran while one was open for 2% of the time, Pallas kernels for 0%

commit v1 on v0

v1 whole, which is shorter than its diff:
```python
import jax
import jax.numpy as jnp
from jax import lax
from jax.experimental import pallas as pl
from jax.experimental.pallas import tpu as pltpu
from jax.sharding import PartitionSpec as P

GROUPS = 32
GN_EPS = 1e-6
MESH = pl.DeviceIdType.MESH
LAG = 4


def solution(mesh):
    rows_n = mesh.shape["sy"]
    cols_n = mesh.shape["sx"]
    tile_spec = P("dp", "sy", "sx", None)
    replicated = P()
    bf16 = jnp.bfloat16
    f32 = jnp.float32

    def make_kernel(samples, tile_h, tile_w):
        lanes = 16
        planes = tile_h // lanes
        ext_w = tile_w + 2
        pairs = planes // 2
        pixel_count = float(tile_h * rows_n * tile_w * cols_n)

        def kernel(act_hbm, params, w_first, w_short, w_rest, w_head, out_ref,
                   a_ext, t_ext, h_ext, a_ud, t_ud, h_ud, act_a, act_m, wp_first, wp_rest,
                   raw, stage_lo, stage_hi, rx1, rx2, rx1a, rx2a,
                   raw_sem, halo_send, halo_recv, st1_send, st1_recv, st2_send, st2_recv):
            my_y = lax.axis_index("sy")
            my_x = lax.axis_index("sx")
            has_up = my_y > 0
            has_down = my_y < rows_n - 1
            has_left = my_x > 0
            has_right = my_x < cols_n - 1

            barrier = pltpu.get_barrier_semaphore()
            for step in range(1, rows_n * cols_n):
                other = lax.rem(my_y * cols_n + my_x + step, rows_n * cols_n)
                pl.semaphore_signal(barrier, inc=1, device_id={"sy": other // cols_n, "sx": lax.rem(other, cols_n)}, device_id_type=MESH)

            def fetch(sample, slot):
                return pltpu.make_async_copy(act_hbm.at[sample], raw.at[slot], raw_sem.at[slot])

            fetch(0, 0).start()

            def pair_weights(dst, src, chans):
                for dc in range(3):
                    for j in range(4):
                        base = (dc * 4 + j) * chans
                        zero = jnp.zeros((chans, 128), bf16)
                        dst[pl.ds(base, chans), 0:128] = src(j, dc) if j < 3 else zero
                        dst[pl.ds(base, chans), 128:256] = src(j - 1, dc) if j > 0 else zero

            pair_weights(wp_first, lambda dr, dc: w_first[dr, dc], 256)

            def pair_rest(index, carry):
                pair_weights(wp_rest.at[index], lambda dr, dc: w_rest[index, dr, dc], 128)
                return carry

            lax.fori_loop(0, 5, pair_rest, 0)

            pl.semaphore_wait(barrier, rows_n * cols_n - 1)

            def halo_copies(ext, ud, parity, sample):
                last = planes - 1
                moves = [
                    (has_left, ext.at[sample, :, 1], ext.at[sample, :, ext_w - 1], my_y, my_x - 1),
                    (has_right, ext.at[sample, :, ext_w - 2], ext.at[sample, :, 0], my_y, my_x + 1),
                    (has_up, ext.at[sample, 0, pl.ds(1, tile_w)], ud.at[1, sample, pl.ds(1, tile_w)], my_y - 1, my_x),
                    (has_down, ext.at[sample, last, pl.ds(1, tile_w)], ud.at[0, sample, pl.ds(1, tile_w)], my_y + 1, my_x),
                    (has_up & has_left, ext.at[sample, 0, 1], ud.at[1, sample, ext_w - 1], my_y - 1, my_x - 1),
                    (has_up & has_right, ext.at[sample, 0, ext_w - 2], ud.at[1, sample, 0], my_y - 1, my_x + 1),
                    (has_down & has_left, ext.at[sample, last, 1], ud.at[0, sample, ext_w - 1], my_y + 1, my_x - 1),
                    (has_down & has_right, ext.at[sample, last, ext_w - 2], ud.at[0, sample, 0], my_y + 1, my_x + 1),
                ]
                return [(cond, pltpu.make_async_remote_copy(
                    src_ref=src, dst_ref=dst, send_sem=halo_send.at[sample, index], recv_sem=halo_recv.at[parity, sample, index],
                    device_id={"sy": to_y, "sx": to_x}, device_id_type=MESH))
                    for index, (cond, src, dst, to_y, to_x) in enumerate(moves)]

            arrivals = [has_right, has_left, has_down, has_up, has_down & has_right, has_down & has_left, has_up & has_right, has_up & has_left]

            def peers(buf, send_sem, recv_sem, parity, sample, along_y):
                mine = my_y if along_y else my_x
                count = rows_n if along_y else cols_n
                copies = []
                for step in range(1, count):
                    to = lax.rem(mine + step, count)
                    copies.append(pltpu.make_async_remote_copy(
                        src_ref=buf.at[parity, sample, mine], dst_ref=buf.at[parity, sample, mine],
                        send_sem=send_sem.at[sample, step], recv_sem=recv_sem.at[parity, sample, step],
                        device_id={"sy": to, "sx": my_x} if along_y else {"sy": my_y, "sx": to}, device_id_type=MESH))
                return copies

            def layer_out(layer):
                if layer == 0:
                    return a_ext, a_ud, 0, rx1a, rx2a
                if layer % 2:
                    return t_ext, t_ud, 1, rx1, rx2
                return h_ext, h_ud, 0, rx1, rx2

            def send_edges(layer, sample):
                ext, ud, parity, sums_one, _ = layer_out(layer)
                for cond, copy in halo_copies(ext, ud, parity, sample):
                    @pl.when(cond)
                    def _(copy=copy):
                        copy.start()
                for copy in peers(sums_one, st1_send, st1_recv, parity, sample, True):
                    copy.start()

            def fold_rows(layer, sample):
                _, _, parity, sums_one, sums_two = layer_out(layer)
                for copy in peers(sums_one, st1_send, st1_recv, parity, sample, True):
                    copy.wait_recv()
                total = sums_one[parity, sample, 0]
                for index in range(1, rows_n):
                    total = total + sums_one[parity, sample, index]
                sums_two[parity, sample, my_x] = total

            def send_rows(layer, sample):
                _, _, parity, _, sums_two = layer_out(layer)
                for copy in peers(sums_two, st2_send, st2_recv, parity, sample, False):
                    copy.start()

            def service(layer, sample):
                @pl.when(sample > 0)
                def _():
                    send_edges(layer, sample - 1)

                @pl.when(sample >= LAG + 1)
                def _():
                    send_rows(layer, sample - LAG - 1)

                @pl.when(sample >= LAG)
                def _():
                    fold_rows(layer, sample - LAG)

                if layer > 0:
                    @pl.when(sample < LAG + 1)
                    def _():
                        send_rows(layer - 1, samples + sample - LAG - 1)

                    @pl.when(sample < LAG)
                    def _():
                        fold_rows(layer - 1, samples + sample - LAG)

            def await_layer(layer, sample):
                ext, ud, parity, sums_one, sums_two = layer_out(layer)
                copies = halo_copies(ext, ud, parity, sample)
                for cond, (_, copy) in zip(arrivals, copies):
                    @pl.when(cond)
                    def _(copy=copy):
                        copy.wait_recv()
                for cond, copy in copies:
                    @pl.when(cond)
                    def _(copy=copy):
                        copy.wait_send()
                for copy in peers(sums_one, st1_send, st1_recv, parity, sample, True):
                    copy.wait_send()
                for copy in peers(sums_two, st2_send, st2_recv, parity, sample, False):
                    copy.wait()

            def group_total(value, per_group):
                lane = lax.broadcasted_iota(jnp.int32, value.shape, 1)
                step = 1
                while step < per_group:
                    ahead = pltpu.roll(value, 128 - step, axis=1)
                    behind = pltpu.roll(value, step, axis=1)
                    value = value + jnp.where(lax.rem(lane, 2 * step) < step, ahead, behind)
                    step *= 2
                return value

            def scale_shift(layer, sample):
                _, _, parity, _, sums_two = layer_out(layer)
                total = sums_two[parity, sample, 0]
                for index in range(1, cols_n):
                    total = total + sums_two[parity, sample, index]
                parts = 2 if layer == 0 else 1
                chans = parts * 128
                per_group = chans // GROUPS
                total = group_total(total, per_group) * (1.0 / (pixel_count * per_group))
                result = []
                for part in range(parts):
                    mean = total[part:part + 1]
                    var = total[parts + part:parts + part + 1] - mean * mean
                    inv = lax.rsqrt(var + GN_EPS)
                    row = part if layer == 0 else 4 + 2 * (layer - 1)
                    gap = 2 if layer == 0 else 1
                    scale = inv * params[row:row + 1, :]
                    shift = params[row + gap:row + gap + 1, :] - mean * scale
                    result.append((0.5 * scale, 0.5 * shift))
                if parts == 1:
                    return result[0]
                return tuple(jnp.concatenate([result[0][i], result[1][i]], axis=1) for i in range(2))

            def activate(layer, sample):
                ext, ud, _, _, _ = layer_out(layer)
                dst = act_a if layer == 0 else act_m
                chans = 256 if layer == 0 else 128
                scale, shift = scale_shift(layer, sample)
                scale3 = scale.reshape(1, 1, chans)
                shift3 = shift.reshape(1, 1, chans)

                def silu(x):
                    half = x.astype(f32) * scale3 + shift3
                    return half + half * jnp.tanh(half)

                for q in range(planes):
                    dst[(q + 1) // 2, (q + 1) % 2, pl.ds(1, tile_w)] = silu(ext[sample, q, pl.ds(1, tile_w)]).astype(bf16)
                for col, cond in ((0, has_left), (ext_w - 1, has_right)):
                    for q in range(planes):
                        value = silu(ext[sample, q, pl.ds(col, 1)])
                        dst[(q + 1) // 2, (q + 1) % 2, pl.ds(col, 1)] = jnp.where(cond, value, 0.0).astype(bf16)
                shape = (ext_w, lanes, chans)
                col_id = lax.broadcasted_iota(jnp.int32, shape, 0)
                row_id = lax.broadcasted_iota(jnp.int32, shape, 1)
                col_lo = jnp.where(has_left, 0, 1)
                col_hi = jnp.where(has_right, ext_w - 1, ext_w - 2)
                in_cols = (col_id >= col_lo) & (col_id <= col_hi)
                for side, cond, near, far, turn, edge in ((0, has_up, planes, 0, 1, 0), (1, has_down, 1, planes + 1, lanes - 1, lanes - 1)):
                    own = pltpu.roll(dst[near // 2, near % 2].astype(f32), turn, axis=1)
                    other = pltpu.roll(silu(ud[side, sample]), turn, axis=1)
                    other = jnp.where(in_cols & cond, other, 0.0)
                    dst[far // 2, far % 2] = jnp.where(row_id == edge, other, own).astype(bf16)

            def convolve(layer, sample):
                src = act_a if layer == 1 else act_m
                chans = 256 if layer == 1 else 128
                ext, _, parity, sums_one, _ = layer_out(layer)
                bias_row = 16 + (layer - 1)
                bias = params[bias_row:bias_row + 1, :]
                if layer == 2:
                    bias = bias + params[22:23, :]
                bias4 = bias.reshape(1, 1, 1, 128)
                weights = wp_first if layer == 1 else wp_rest.at[layer - 2]
                sum_one = jnp.zeros((8, 128), f32)
                sum_two = jnp.zeros((8, 128), f32)
                parts = 2
                span = pairs // parts
                for part in range(parts):
                    pieces = []
                    for dc in range(3):
                        for j in range(4):
                            piece = src[pl.ds(part * span + j // 2, span), j % 2, pl.ds(dc, tile_w)]
                            pieces.append(piece.reshape(span * tile_w * lanes, chans))
                    accum = jnp.dot(jnp.concatenate(pieces, axis=1), weights[...], preferred_element_type=f32)
                    for k in range(span):
                        for odd in range(2):
                            q = 2 * (part * span + k) + odd
                            value = accum[k * 128:(k + 1) * 128, odd * 128:(odd + 1) * 128].reshape(tile_w, lanes, 128) + bias.reshape(1, 1, 128)
                            if layer == 2:
                                skip = jnp.dot(a_ext[sample, q, pl.ds(1, tile_w)].reshape(128, 256), w_short[...], preferred_element_type=f32)
                                value = value + skip.reshape(tile_w, lanes, 128)
                            elif layer % 2 == 0:
                                value = value + ext[sample, q, pl.ds(1, tile_w)].astype(f32)
                            value = value.astype(bf16)
                            ext[sample, q, pl.ds(1, tile_w)] = value
                            wide = value.astype(f32).reshape(tile_w * 2, 8, 128)
                            sum_one = sum_one + jnp.sum(wide, axis=0)
                            sum_two = sum_two + jnp.sum(wide * wide, axis=0)
                sums_one[parity, sample, my_y] = jnp.concatenate(
                    [jnp.sum(sum_one, axis=0, keepdims=True), jnp.sum(sum_two, axis=0, keepdims=True)], axis=0)

            def load_step(sample, carry):
                slot = lax.rem(sample, 2)
                fetch(sample, slot).wait()

                @pl.when(sample + 1 < samples)
                def _():
                    fetch(sample + 1, 1 - slot).start()

                service(0, sample)
                for chunk in range(tile_h // 16):
                    piece = raw[slot, pl.ds(chunk * 16, 16)].astype(f32).reshape(16 * tile_w, 256)
                    stage_lo[pl.ds(chunk * 16 * tile_w, 16 * tile_w), :] = piece[:, :128]
                    stage_hi[pl.ds(chunk * 16 * tile_w, 16 * tile_w), :] = piece[:, 128:]
                for half, stage in ((0, stage_lo), (1, stage_hi)):
                    sum_one = jnp.zeros((lanes, 128), f32)
                    sum_two = jnp.zeros((lanes, 128), f32)
                    for q in range(planes):
                        for c in range(tile_w):
                            value = stage[pl.ds(q * tile_w + c, lanes, stride=planes * tile_w), :]
                            a_ext[sample, q, c + 1, :, half * 128:(half + 1) * 128] = value.astype(bf16)
                            sum_one = sum_one + value
                            sum_two = sum_two + value * value
                    rx1a[0, sample, my_y, half:half + 1] = jnp.sum(sum_one, axis=0, keepdims=True)
                    rx1a[0, sample, my_y, half + 2:half + 3] = jnp.sum(sum_two, axis=0, keepdims=True)
                return carry

            lax.fori_loop(0, samples, load_step, 0)
            send_edges(0, samples - 1)

            for layer in range(1, 7):
                def conv_step(sample, carry, layer=layer):
                    service(layer, sample)
                    await_layer(layer - 1, sample)
                    activate(layer - 1, sample)
                    convolve(layer, sample)
                    return carry

                lax.fori_loop(0, samples, conv_step, 0)
                send_edges(layer, samples - 1)

            def head_step(sample, carry):
                @pl.when(sample < LAG + 1)
                def _():
                    send_rows(6, samples + sample - LAG - 1)

                @pl.when(sample < LAG)
                def _():
                    fold_rows(6, samples + sample - LAG)

                await_layer(6, sample)
                activate(6, sample)
                flat = act_m[...].reshape((planes + 2) * ext_w * lanes, 128)
                width = out_ref.shape[2]
                flat = jnp.concatenate([flat, jnp.zeros((width - flat.shape[0], 128), bf16)], axis=0)
                taps = lax.dot_general(w_head[...], flat, (((1,), (1,)), ((), ())), preferred_element_type=f32)
                image = taps[0:8]
                for tap in range(1, 9):
                    offset = ((tap // 3) * ext_w + tap % 3) * lanes
                    image = image + pltpu.roll(taps[8 * tap:8 * tap + 8], width - offset, axis=1)
                out_ref[sample] = image
                return carry

            lax.fori_loop(0, samples, head_step, 0)

        return kernel, lanes, planes, ext_w

    def local_decode(act_in, norm_first, w_first, w_short, norm_rest, w_rest, bias_rest, w_out, bias_out):
        samples, tile_h, tile_w, _ = act_in.shape
        kernel, lanes, planes, ext_w = make_kernel(samples, tile_h, tile_w)
        params = jnp.concatenate([norm_first.reshape(4, 128), norm_rest.reshape(12, 128), bias_rest, jnp.zeros((1, 128), bf16)], axis=0).astype(f32)
        w_head = jnp.pad(w_out.transpose(0, 1, 3, 2).reshape(9, 3, 128), ((0, 0), (0, 5), (0, 0))).reshape(72, 128)
        width = -(-((planes + 2) * ext_w * lanes) // 128) * 128
        vmem = pl.BlockSpec(memory_space=pltpu.VMEM)
        scratch = [
            pltpu.VMEM((samples, planes, ext_w, lanes, 256), bf16),
            pltpu.VMEM((samples, planes, ext_w, lanes, 128), bf16),
            pltpu.VMEM((samples, planes, ext_w, lanes, 128), bf16),
            pltpu.VMEM((2, samples, ext_w, lanes, 256), bf16),
            pltpu.VMEM((2, samples, ext_w, lanes, 128), bf16),
            pltpu.VMEM((2, samples, ext_w, lanes, 128), bf16),
            pltpu.VMEM(((planes + 2) // 2, 2, ext_w, lanes, 256), bf16),
            pltpu.VMEM(((planes + 2) // 2, 2, ext_w, lanes, 128), bf16),
            pltpu.VMEM((12 * 256, 256), bf16),
            pltpu.VMEM((5, 12 * 128, 256), bf16),
            pltpu.VMEM((2, tile_h, tile_w, 256), bf16),
            pltpu.VMEM((tile_h * tile_w, 128), f32),
            pltpu.VMEM((tile_h * tile_w, 128), f32),
            pltpu.VMEM((2, samples, rows_n, 2, 128), f32),
            pltpu.VMEM((2, samples, cols_n, 2, 128), f32),
            pltpu.VMEM((1, samples, rows_n, 4, 128), f32),
            pltpu.VMEM((1, samples, cols_n, 4, 128), f32),
            pltpu.SemaphoreType.DMA((2,)),
            pltpu.SemaphoreType.DMA((samples, 8)),
            pltpu.SemaphoreType.DMA((2, samples, 8)),
            pltpu.SemaphoreType.DMA((samples, rows_n)),
            pltpu.SemaphoreType.DMA((2, samples, rows_n)),
            pltpu.SemaphoreType.DMA((samples, cols_n)),
            pltpu.SemaphoreType.DMA((2, samples, cols_n)),
        ]
        image = pl.pallas_call(
            kernel,
            out_shape=jax.ShapeDtypeStruct((samples, 8, width), f32),
            in_specs=[pl.BlockSpec(memory_space=pl.ANY), vmem, vmem, vmem, vmem, vmem],
            out_specs=vmem,
            scratch_shapes=scratch,
            compiler_params=pltpu.CompilerParams(collective_id=0, has_side_effects=True, vmem_limit_bytes=60 * 1024 * 1024),
        )(act_in, params, w_first, w_short, w_rest, w_head)
        image = image[:, :3, :planes * ext_w * lanes].reshape(samples, 3, planes, ext_w, lanes)[:, :, :, :tile_w]
        image = image.transpose(0, 4, 2, 3, 1).reshape(samples, tile_h, tile_w, 3)
        return image + bias_out.astype(f32)

    return jax.shard_map(local_decode, mesh=mesh, in_specs=(tile_spec, replicated, replicated, replicated, replicated, replicated, replicated, replicated, replicated), out_specs=tile_spec, check_vma=False)
```

time: 1010 us -> 193 us (0.19)
  blocking collectives: 413 us -> 0 us
  matrix products: 277 us -> 0 us
  Pallas kernels: 0 us -> 176 us
  waiting for transfers between devices: 163 us -> 0 us
  other arithmetic: 91 us -> 2.16 us
  starting transfers between devices: 41.3 us -> 0 us
    psum x7 -> x0, blocking collectives: 413 us -> none  [group_norm_act(): totals = lax.psum(jnp.stack([sum_one, sum_two], axis=-1), ('sy', 'sx'))]
    conv_general_dilated x7 -> x0, matrix products: 265 us -> none  [conv_tile(): lax.conv_general_dilated(add_border(act_map), kernel, (1, 1), ((0, 0), (0...]
    pallas_call x0 -> x1, Pallas kernels: none -> 176 us  [local_decode(): pl.pallas_call(kernel, out_shape=jax.ShapeDtypeStruct((samples, 8, width)...]
    ppermute x28 -> x0, waiting for transfers between devices: 163 us -> none  [the longest x7 107 us: add_border(): left_col = lax.ppermute(tall[:, :, -1:], 'sx', to_right)]
    convert_element_type x10 -> x2, other arithmetic: 66.8 us -> 1.35 us  [the longest x1 1.35 us: local_decode(): jnp.concatenate([norm_first.reshape(4, 128), norm_rest.reshape(12, 128),...]
    ppermute x28 -> x0, starting transfers between devices: 41.3 us -> none  [the longest x7 11.5 us: add_border(): left_col = lax.ppermute(tall[:, :, -1:], 'sx', to_right)]
    reduce_sum x15 -> x0, other arithmetic: 20.5 us -> none  [the longest x8 20.1 us: group_norm_act(): jnp.sum(act_map, axis=(1, 2), dtype=jnp.float32)]
    dot_general x1 -> x0, matrix products: 12.6 us -> none  [local_decode(): jnp.einsum('nhwc,cd->nhwd', act_in, w_short, preferred_element_type=jnp.f...]
  transfers between devices with their start and end apart: 28 -> 0, of which waited for: 21 -> 0; matrix products, arithmetic and copies ran while one was open for 2% -> 0% of each run, Pallas kernels for 0% -> 0%
where the time goes in v1:
time: 193 us; the launch traced here: 192 us
  Pallas kernels  176 us (91%)
  local copies, waits for them, and re-layouts  14.2 us (7%)
  other arithmetic  2.16 us (1%)
    pallas_call x1, Pallas kernels, local_decode(): pl.pallas_call(kernel, out_shape=jax.ShapeDtypeStruct((samples, 8, width)...  176 us

profile of v1, /device:TPU:0, one launch (start us, length us, event | category | flops | bytes accessed | tf_op | source)
XLA Modules:
  0.0 192.3 jit_solution(6394974229630121539)
XLA Ops:
  0.0 1.3 pad_bitcast_fusion.w_head
  1.3 0.7 reshape.20
  2.0 0.7 reshape.19
  2.7 0.1 pad.8.clone
  2.8 1.3 maximum_convert_fusion.params
  4.1 175.9 %shard_map.91 = f32[12,8,2944]{2,1,0:T(8,128)} custom-call(bf16[12,256,8,256]{3,2,1,0:T(8,128)(2,1)} %act_hbm.1, f32[24,128]{1,0:T(8,128)} %maximum_convert_fusion.params, bf16[3,3,256,128]{3,2,1,0:T(8,128)(2,1)} %w_first.1, bf16[256,128]{1,0:T(8,128)(2,1)} %w_short.1, bf16[5,3,3,128,128]{4,3,2,1,0:T(8,128)(2,1)} %w_rest.1, ...), custom_call_target="tpu_custom_call" | custom-call | tf_op jit(solution)/shard_map/pallas_call | solution.py:367
  180.0 1.3 slice.6
  181.3 0.1 copy.12
  181.4 3.7 %reshape.23 = f32[12,3,16,10,16]{4,3,2,0,1:T(8,128)} reshape(f32[12,3,2560]{2,0,1:T(8,128)S(1)} %copy.12) | data formatting | bytes 737280 | tf_op jit(solution)/shard_map/reshape | solution.py:375
  185.1 1.8 slice_bitcast_fusion
  186.9 2.0 %copy.13 = f32[12,16,16,8,3]{2,1,3,4,0:T(8,128)} copy(f32[12,16,16,8,3]{1,3,2,0,4:T(8,128)S(1)} %slice_bitcast_fusion) | data formatting | bytes 589824 | tf_op jit(solution)/shard_map/transpose | solution.py:376
  188.9 0.0 copy-start
  188.9 2.5 %reshape.24 = f32[12,256,8,3]{1,2,3,0:T(8,128)S(1)} reshape(f32[12,16,16,8,3]{2,1,3,4,0:T(8,128)} %copy.13) | data formatting | bytes 589824 | tf_op jit(solution)/shard_map/reshape | solution.py:376
  191.4 0.0 copy-done
  191.5 0.8 broadcast_add_fusion
  (1 shorter events, 0.0 us)
Async XLA Ops:
  188.9 2.5 %copy-start = (bf16[3]{0:T(256)(128)(2,1)S(1)}, bf16[3]{0:T(256)(128)(2,1)}, u32[]{:S(2)}) copy-start(bf16[3]{0:T(256)(128)(2,1)} %param.17) | copy-start | bytes 22

commit v2 on v1

v2 whole, which is shorter than its diff:
```python
import jax
import jax.numpy as jnp
from jax import lax
from jax.experimental import pallas as pl
from jax.experimental.pallas import tpu as pltpu
from jax.sharding import PartitionSpec as P

GROUPS = 32
GN_EPS = 1e-6
MESH = pl.DeviceIdType.MESH
BATCH = 3


def solution(mesh):
    rows_n = mesh.shape["sy"]
    cols_n = mesh.shape["sx"]
    tile_spec = P("dp", "sy", "sx", None)
    replicated = P()
    bf16 = jnp.bfloat16
    f32 = jnp.float32

    def make_kernel(samples, tile_h, tile_w):
        lanes = 16
        planes = tile_h // lanes
        ext_w = tile_w + 2
        pairs = planes // 2
        pixel_count = float(tile_h * rows_n * tile_w * cols_n)

        batches = samples // BATCH
        column_lanes = (planes + 2) * lanes
        flat_width = -(-(ext_w * column_lanes) // 128) * 128

        def kernel(act_hbm, norm_first, norm_rest, bias_rest, bias_out, w_first, w_short, w_rest, w_out, out_ref,
                   a_ext, t_ext, h_ext, a_ud, t_ud, h_ud, act_a, act_m, wp_first, wp_rest, w_head, reorder, image_rows,
                   raw, stage_lo, stage_hi, rx1, rx2, rx1a, rx2a,
                   raw_sem, col_send, col_recv, row_send, row_recv, st1_send, st1_recv, st2_send, st2_recv):
            my_y = lax.axis_index("sy")
            my_x = lax.axis_index("sx")
            has_up = my_y > 0
            has_down = my_y < rows_n - 1
            has_left = my_x > 0
            has_right = my_x < cols_n - 1

            barrier = pltpu.get_barrier_semaphore()
            for step in range(1, rows_n * cols_n):
                other = lax.rem(my_y * cols_n + my_x + step, rows_n * cols_n)
                pl.semaphore_signal(barrier, inc=1, device_id={"sy": other // cols_n, "sx": lax.rem(other, cols_n)}, device_id_type=MESH)

            def fetch(sample, slot):
                return pltpu.make_async_copy(act_hbm.at[sample], raw.at[slot], raw_sem.at[slot])

            fetch(0, 0).start()

            def pair_weights(dst, src, chans):
                for dc in range(3):
                    for j in range(4):
                        base = (dc * 4 + j) * chans
                        zero = jnp.zeros((chans, 128), bf16)
                        dst[pl.ds(base, chans), 0:128] = src(j, dc) if j < 3 else zero
                        dst[pl.ds(base, chans), 128:256] = src(j - 1, dc) if j > 0 else zero

            pair_weights(wp_first, lambda dr, dc: w_first[dr, dc], 256)

            def pair_rest(index, carry):
                pair_weights(wp_rest.at[index], lambda dr, dc: w_rest[index, dr, dc], 128)
                return carry

            lax.fori_loop(0, 5, pair_rest, 0)

            for tap in range(9):
                taps3 = w_out[tap // 3, tap % 3].astype(f32)
                w_head[pl.ds(8 * tap, 8), :] = jnp.concatenate([taps3, jnp.zeros((5, 128), f32)], axis=0)
            from_id = lax.broadcasted_iota(jnp.int32, (tile_h, tile_h), 0)
            to_id = lax.broadcasted_iota(jnp.int32, (tile_h, tile_h), 1)
            reorder[...] = jnp.where(lax.rem(from_id, lanes) * planes + from_id // lanes == to_id, 1.0, 0.0).astype(bf16)

            pl.semaphore_wait(barrier, rows_n * cols_n - 1)

            def span(batch):
                return pl.ds(batch * BATCH, BATCH)

            def remote(src, dst, send_sem, recv_sem, to_y, to_x):
                return pltpu.make_async_remote_copy(src_ref=src, dst_ref=dst, send_sem=send_sem, recv_sem=recv_sem,
                                                    device_id={"sy": to_y, "sx": to_x}, device_id_type=MESH)

            def column_copies(ext, parity, sample):
                moves = [(has_left, has_right, 1, ext_w - 1, my_x - 1), (has_right, has_left, ext_w - 2, 0, my_x + 1)]
                return [(leaves, arrives, remote(ext.at[sample, :, src], ext.at[sample, :, dst], col_send.at[sample, index], col_recv.at[parity, sample, index], my_y, to_x))
                        for index, (leaves, arrives, src, dst, to_x) in enumerate(moves)]

            def row_copies(ext, ud, parity, batch):
                moves = [(has_up, has_down, 0, 1, my_y - 1), (has_down, has_up, planes - 1, 0, my_y + 1)]
                return [(leaves, arrives, remote(ext.at[span(batch), src], ud.at[side, span(batch)], row_send.at[batch, side], row_recv.at[parity, batch, side], to_y, my_x))
                        for leaves, arrives, src, side, to_y in moves]

            def peers(buf, send_sem, recv_sem, parity, batch, along_y):
                mine = my_y if along_y else my_x
                count = rows_n if along_y else cols_n
                copies = []
                for step in range(1, count):
                    to = lax.rem(mine + step, count)
                    slot = buf.at[parity, batch, mine]
                    copies.append(remote(slot, slot, send_sem.at[batch, step], recv_sem.at[parity, batch, step], to if along_y else my_y, my_x if along_y else to))
                return copies

            def layer_out(layer):
                if layer == 0:
                    return a_ext, a_ud, 0, rx1a, rx2a
                if layer % 2:
                    return t_ext, t_ud, 1, rx1, rx2
                return h_ext, h_ud, 0, rx1, rx2

            def start_if(cond, copy):
                @pl.when(cond)
                def _():
                    copy.start()

            def send_columns(layer, sample):
                ext, _, parity, _, _ = layer_out(layer)
                for leaves, _, copy in column_copies(ext, parity, sample):
                    start_if(leaves, copy)

            def send_sums(layer, batch):
                _, _, parity, sums_one, _ = layer_out(layer)
                for copy in peers(sums_one, st1_send, st1_recv, parity, batch, True):
                    copy.start()

            def pass_on(layer, batch):
                ext, ud, parity, sums_one, sums_two = layer_out(layer)
                for index in range(BATCH):
                    for _, arrives, copy in column_copies(ext, parity, batch * BATCH + index):
                        @pl.when(arrives)
                        def _(copy=copy):
                            copy.wait_recv()
                for leaves, _, copy in row_copies(ext, ud, parity, batch):
                    start_if(leaves, copy)
                for copy in peers(sums_one, st1_send, st1_recv, parity, batch, True):
                    copy.wait_recv()
                total = sums_one[parity, batch, 0]
                for index in range(1, rows_n):
                    total = total + sums_one[parity, batch, index]
                parts = 2 if layer == 0 else 1
                for index in range(BATCH):
                    sums_two[parity, batch, my_x, index] = pack_groups(total[index], parts)

            def send_totals(layer, batch):
                _, _, parity, _, sums_two = layer_out(layer)
                for copy in peers(sums_two, st2_send, st2_recv, parity, batch, False):
                    copy.start()

            def boundary(layer, batch):
                @pl.when(batch > 0)
                def _():
                    send_sums(layer, batch - 1)

                @pl.when(batch >= 2)
                def _():
                    pass_on(layer, batch - 2)

                if layer > 0:
                    @pl.when(batch < 2)
                    def _():
                        pass_on(layer - 1, batches + batch - 2)

            def within(layer, batch, index):
                @pl.when((index == 1) & (batch >= 2))
                def _():
                    send_totals(layer, batch - 2)

                if layer > 0:
                    @pl.when((index == 1) & (batch < 2))
                    def _():
                        send_totals(layer - 1, batches + batch - 2)

            def await_batch(layer, batch):
                ext, ud, parity, sums_one, sums_two = layer_out(layer)
                rows = row_copies(ext, ud, parity, batch)
                for _, arrives, copy in rows:
                    @pl.when(arrives)
                    def _(copy=copy):
                        copy.wait_recv()
                for leaves, _, copy in rows:
                    @pl.when(leaves)
                    def _(copy=copy):
                        copy.wait_send()
                for index in range(BATCH):
                    for leaves, _, copy in column_copies(ext, parity, batch * BATCH + index):
                        @pl.when(leaves)
                        def _(copy=copy):
                            copy.wait_send()
                for copy in peers(sums_one, st1_send, st1_recv, parity, batch, True):
                    copy.wait_send()
                for copy in peers(sums_two, st2_send, st2_recv, parity, batch, False):
                    copy.wait()

            def group_total(value, per_group):
                lane = lax.broadcasted_iota(jnp.int32, value.shape, 1)
                step = 1
                while step < per_group:
                    ahead = pltpu.roll(value, 128 - step, axis=1)
                    behind = pltpu.roll(value, step, axis=1)
                    value = value + jnp.where(lax.rem(lane, 2 * step) < step, ahead, behind)
                    step *= 2
                return value

            def pack_groups(sums, parts):
                rows = 2 * parts
                groups = group_total(sums, 128 * parts // GROUPS)
                lane = lax.rem(lax.broadcasted_iota(jnp.int32, (1, 128), 1), rows)
                packed = groups[0:1]
                for row in range(1, rows):
                    packed = jnp.where(lane == row, groups[row:row + 1], packed)
                return packed

            def unpack_groups(packed, parts):
                rows = 2 * parts
                lane = lax.rem(lax.broadcasted_iota(jnp.int32, (1, 128), 1), rows)
                return [group_total(jnp.where(lane == row, packed, 0.0), rows) for row in range(rows)]

            def scale_shift(layer, sample):
                _, _, parity, _, sums_two = layer_out(layer)
                batch, index = sample // BATCH, lax.rem(sample, BATCH)
                total = sums_two[parity, batch, 0, index]
                for source in range(1, cols_n):
                    total = total + sums_two[parity, batch, source, index]
                parts = 2 if layer == 0 else 1
                moments = unpack_groups(total * (1.0 / (pixel_count * (128 * parts // GROUPS))), parts)
                pair = (norm_first[...] if layer == 0 else norm_rest[layer - 1]).astype(f32)
                result = []
                for part in range(parts):
                    mean, square = moments[part], moments[parts + part]
                    inv = lax.rsqrt(square - mean * mean + GN_EPS)
                    scale = inv * pair[0:1, part * 128:(part + 1) * 128]
                    shift = pair[1:2, part * 128:(part + 1) * 128] - mean * scale
                    result.append((0.5 * scale, 0.5 * shift))
                if parts == 1:
                    return result[0]
                return tuple(jnp.concatenate([result[0][i], result[1][i]], axis=1) for i in range(2))

            def activate(layer, sample):
                ext, ud, _, _, _ = layer_out(layer)
                dst = act_a if layer == 0 else act_m
                chans = 256 if layer == 0 else 128
                scale, shift = scale_shift(layer, sample)
                scale3 = scale.reshape(1, 1, chans)
                shift3 = shift.reshape(1, 1, chans)

                def silu(x):
                    half = x.astype(f32) * scale3 + shift3
                    return half + half * jnp.tanh(half)

                for q in range(planes):
                    dst[(q + 1) // 2, (q + 1) % 2, pl.ds(1, tile_w)] = silu(ext[sample, q, pl.ds(1, tile_w)]).astype(bf16)
                for col, cond in ((0, has_left), (ext_w - 1, has_right)):
                    for q in range(planes):
                        value = silu(ext[sample, q, pl.ds(col, 1)])
                        dst[(q + 1) // 2, (q + 1) % 2, pl.ds(col, 1)] = jnp.where(cond, value, 0.0).astype(bf16)
                shape = (ext_w, lanes, chans)
                col_id = lax.broadcasted_iota(jnp.int32, shape, 0)
                row_id = lax.broadcasted_iota(jnp.int32, shape, 1)
                col_lo = jnp.where(has_left, 0, 1)
                col_hi = jnp.where(has_right, ext_w - 1, ext_w - 2)
                in_cols = (col_id >= col_lo) & (col_id <= col_hi)
                for side, cond, near, far, turn, edge in ((0, has_up, planes, 0, 1, 0), (1, has_down, 1, planes + 1, lanes - 1, lanes - 1)):
                    own = pltpu.roll(dst[near // 2, near % 2].astype(f32), turn, axis=1)
                    other = pltpu.roll(silu(ud[side, sample]), turn, axis=1)
                    other = jnp.where(in_cols & cond, other, 0.0)
                    dst[far // 2, far % 2] = jnp.where(row_id == edge, other, own).astype(bf16)

            def convolve(layer, sample):
                src = act_a if layer == 1 else act_m
                chans = 256 if layer == 1 else 128
                ext, _, parity, sums_one, _ = layer_out(layer)
                bias_rows = bias_rest[...].astype(f32)
                bias = bias_rows[layer - 1:layer]
                if layer == 2:
                    bias = bias + bias_rows[6:7]
                weights = wp_first if layer == 1 else wp_rest.at[layer - 2]
                sum_one = jnp.zeros((8, 128), f32)
                sum_two = jnp.zeros((8, 128), f32)
                parts = 2
                half = pairs // parts
                for part in range(parts):
                    pieces = []
                    for dc in range(3):
                        for j in range(4):
                            piece = src[pl.ds(part * half + j // 2, half), j % 2, pl.ds(dc, tile_w)]
                            pieces.append(piece.reshape(half * tile_w * lanes, chans))
                    accum = jnp.dot(jnp.concatenate(pieces, axis=1), weights[...], preferred_element_type=f32)
                    for k in range(half):
                        for odd in range(2):
                            q = 2 * (part * half + k) + odd
                            value = accum[k * 128:(k + 1) * 128, odd * 128:(odd + 1) * 128].reshape(tile_w, lanes, 128) + bias.reshape(1, 1, 128)
                            if layer == 2:
                                skip = jnp.dot(a_ext[sample, q, pl.ds(1, tile_w)].reshape(128, 256), w_short[...], preferred_element_type=f32)
                                value = value + skip.reshape(tile_w, lanes, 128)
                            elif layer % 2 == 0:
                                value = value + ext[sample, q, pl.ds(1, tile_w)].astype(f32)
                            value = value.astype(bf16)
                            ext[sample, q, pl.ds(1, tile_w)] = value
                            wide = value.astype(f32).reshape(tile_w * 2, 8, 128)
                            sum_one = sum_one + jnp.sum(wide, axis=0)
                            sum_two = sum_two + jnp.sum(wide * wide, axis=0)
                sums_one[parity, sample // BATCH, my_y, lax.rem(sample, BATCH)] = jnp.concatenate(
                    [jnp.sum(sum_one, axis=0, keepdims=True), jnp.sum(sum_two, axis=0, keepdims=True)], axis=0)

            def load_step(index, batch):
                sample = batch * BATCH + index
                slot = lax.rem(sample, 2)
                fetch(sample, slot).wait()

                @pl.when(sample + 1 < samples)
                def _():
                    fetch(sample + 1, 1 - slot).start()

                @pl.when(sample > 0)
                def _():
                    send_columns(0, sample - 1)

                within(0, batch, index)
                for chunk in range(tile_h // 16):
                    piece = raw[slot, pl.ds(chunk * 16, 16)].astype(f32).reshape(16 * tile_w, 256)
                    stage_lo[pl.ds(chunk * 16 * tile_w, 16 * tile_w), :] = piece[:, :128]
                    stage_hi[pl.ds(chunk * 16 * tile_w, 16 * tile_w), :] = piece[:, 128:]
                for half, stage in ((0, stage_lo), (1, stage_hi)):
                    sum_one = jnp.zeros((lanes, 128), f32)
                    sum_two = jnp.zeros((lanes, 128), f32)
                    for q in range(planes):
                        for c in range(tile_w):
                            value = stage[pl.ds(q * tile_w + c, lanes, stride=planes * tile_w), :]
                            a_ext[sample, q, c + 1, :, half * 128:(half + 1) * 128] = value.astype(bf16)
                            sum_one = sum_one + value
                            sum_two = sum_two + value * value
                    rx1a[0, sample // BATCH, my_y, lax.rem(sample, BATCH), half:half + 1] = jnp.sum(sum_one, axis=0, keepdims=True)
                    rx1a[0, sample // BATCH, my_y, lax.rem(sample, BATCH), half + 2:half + 3] = jnp.sum(sum_two, axis=0, keepdims=True)
                return batch

            def load_batch(batch, carry):
                boundary(0, batch)
                lax.fori_loop(0, BATCH, load_step, batch)
                return carry

            lax.fori_loop(0, batches, load_batch, 0)
            send_columns(0, samples - 1)
            send_sums(0, batches - 1)

            for layer in range(1, 7):
                def conv_step(index, batch, layer=layer):
                    sample = batch * BATCH + index

                    @pl.when(sample > 0)
                    def _():
                        send_columns(layer, sample - 1)

                    within(layer, batch, index)
                    activate(layer - 1, sample)
                    convolve(layer, sample)
                    return batch

                def conv_batch(batch, carry, layer=layer, conv_step=conv_step):
                    boundary(layer, batch)
                    await_batch(layer - 1, batch)
                    lax.fori_loop(0, BATCH, conv_step, batch)
                    return carry

                lax.fori_loop(0, batches, conv_batch, 0)
                send_columns(layer, samples - 1)
                send_sums(layer, batches - 1)

            def head_step(index, batch):
                sample = batch * BATCH + index

                @pl.when((index == 1) & (batch < 2))
                def _():
                    send_totals(6, batches + batch - 2)

                activate(6, sample)
                flat = jnp.swapaxes(act_m[...].reshape(planes + 2, ext_w, lanes, 128), 0, 1).reshape(ext_w * column_lanes, 128)
                flat = jnp.concatenate([flat, jnp.zeros((flat_width - flat.shape[0], 128), bf16)], axis=0)
                taps = lax.dot_general(w_head[...].astype(bf16), flat, (((1,), (1,)), ((), ())), preferred_element_type=f32)
                image = taps[0:8]
                for tap in range(1, 9):
                    offset = (tap % 3) * column_lanes + (tap // 3) * lanes
                    image = image + pltpu.roll(taps[8 * tap:8 * tap + 8], flat_width - offset, axis=1)
                rest = jnp.concatenate([image[:, c * column_lanes:c * column_lanes + tile_h] for c in range(tile_w)], axis=0)
                moved = jnp.zeros(rest.shape, f32)
                for _ in range(3):
                    piece = rest.astype(bf16)
                    moved = moved + jnp.dot(piece, reorder[...], preferred_element_type=f32)
                    rest = rest - piece.astype(f32)
                for side in range(tile_h // 128):
                    image_rows[side] = moved[:, side * 128:(side + 1) * 128]
                for chan in range(3):
                    for side in range(tile_h // 128):
                        out_ref[sample, chan, :, side * 128:(side + 1) * 128] = image_rows[side, pl.ds(chan, tile_w, stride=8), :] + bias_out[chan]
                return batch

            def head_batch(batch, carry):
                @pl.when(batch < 2)
                def _():
                    pass_on(6, batches + batch - 2)

                await_batch(6, batch)
                lax.fori_loop(0, BATCH, head_step, batch)
                return carry

            lax.fori_loop(0, batches, head_batch, 0)

        return kernel, lanes, planes, ext_w

    def local_decode(act_in, norm_first, w_first, w_short, norm_rest, w_rest, bias_rest, w_out, bias_out):
        samples, tile_h, tile_w, _ = act_in.shape
        kernel, lanes, planes, ext_w = make_kernel(samples, tile_h, tile_w)
        batches = samples // BATCH
        vmem = pl.BlockSpec(memory_space=pltpu.VMEM)
        scratch = [
            pltpu.VMEM((samples, planes, ext_w, lanes, 256), bf16),
            pltpu.VMEM((samples, planes, ext_w, lanes, 128), bf16),
            pltpu.VMEM((samples, planes, ext_w, lanes, 128), bf16),
            pltpu.VMEM((2, samples, ext_w, lanes, 256), bf16),
            pltpu.VMEM((2, samples, ext_w, lanes, 128), bf16),
            pltpu.VMEM((2, samples, ext_w, lanes, 128), bf16),
            pltpu.VMEM(((planes + 2) // 2, 2, ext_w, lanes, 256), bf16),
            pltpu.VMEM(((planes + 2) // 2, 2, ext_w, lanes, 128), bf16),
            pltpu.VMEM((12 * 256, 256), bf16),
            pltpu.VMEM((5, 12 * 128, 256), bf16),
            pltpu.VMEM((72, 128), f32),
            pltpu.VMEM((tile_h, tile_h), bf16),
            pltpu.VMEM((tile_h // 128, 8 * tile_w, 128), f32),
            pltpu.VMEM((2, tile_h, tile_w, 256), bf16),
            pltpu.VMEM((tile_h * tile_w, 128), f32),
            pltpu.VMEM((tile_h * tile_w, 128), f32),
            pltpu.VMEM((2, batches, rows_n, BATCH, 2, 128), f32),
            pltpu.VMEM((2, batches, cols_n, BATCH, 1, 128), f32),
            pltpu.VMEM((1, batches, rows_n, BATCH, 4, 128), f32),
            pltpu.VMEM((1, batches, cols_n, BATCH, 1, 128), f32),
            pltpu.SemaphoreType.DMA((2,)),
            pltpu.SemaphoreType.DMA((samples, 2)),
            pltpu.SemaphoreType.DMA((2, samples, 2)),
            pltpu.SemaphoreType.DMA((batches, 2)),
            pltpu.SemaphoreType.DMA((2, batches, 2)),
            pltpu.SemaphoreType.DMA((batches, rows_n)),
            pltpu.SemaphoreType.DMA((2, batches, rows_n)),
            pltpu.SemaphoreType.DMA((batches, cols_n)),
            pltpu.SemaphoreType.DMA((2, batches, cols_n)),
        ]
        image = pl.pallas_call(
            kernel,
            out_shape=jax.ShapeDtypeStruct((samples, 3, tile_w, tile_h), f32),
            in_specs=[pl.BlockSpec(memory_space=pl.ANY), vmem, vmem, vmem, pl.BlockSpec(memory_space=pltpu.SMEM), vmem, vmem, vmem, vmem],
            out_specs=vmem,
            scratch_shapes=scratch,
            compiler_params=pltpu.CompilerParams(collective_id=0, has_side_effects=True, vmem_limit_bytes=60 * 1024 * 1024),
        )(act_in, norm_first, norm_rest, bias_rest, bias_out.astype(f32), w_first, w_short, w_rest, w_out.transpose(0, 1, 3, 2))
        return image.transpose(0, 3, 2, 1)

    return jax.shard_map(local_decode, mesh=mesh, in_specs=(tile_spec, replicated, replicated, replicated, replicated, replicated, replicated, replicated, replicated), out_specs=tile_spec, check_vma=False)
```

time: 193 us -> 173 us (0.90)
  local copies, waits for them, and re-layouts: 14.2 us -> 1.69 us
  Pallas kernels: 176 us -> 170 us
    reshape x5 -> x0, local copies, waits for them, and re-layouts: 8.96 us -> none  [the longest x1 3.71 us: local_decode(): image[:, :3, :planes * ext_w * lanes]]
    pallas_call x1, Pallas kernels: 176 us -> 170 us  [local_decode(): pl.pallas_call(kernel, out_shape=jax.ShapeDtypeStruct((samples, 3, tile_w...]
    transpose x2 -> x0, local copies, waits for them, and re-layouts: 3.79 us -> none  [local_decode(): image = image.transpose(0, 4, 2, 3, 1).reshape(samples, tile_h, tile_w, 3)]
where the time goes in v2:
time: 173 us
  Pallas kernels  170 us (98%)
    pallas_call x1, Pallas kernels, local_decode(): pl.pallas_call(kernel, out_shape=jax.ShapeDtypeStruct((samples, 3, tile_w...  170 us

profile of v2, /device:TPU:0, one launch (start us, length us, event | category | flops | bytes accessed | tf_op | source)
XLA Modules:
  0.0 172.7 jit_solution(1854976815085198370)
XLA Ops:
  0.0 1.2 convert_element_type.3.bias_out
  1.2 169.8 %shard_map.91 = f32[12,3,8,256]{3,2,1,0:T(8,128)} custom-call(bf16[12,256,8,256]{3,2,1,0:T(8,128)(2,1)} %act_hbm.1, bf16[2,256]{1,0:T(2,128)(2,1)} %norm_first.1, bf16[6,2,128]{2,1,0:T(2,128)(2,1)} %norm_rest.1, bf16[7,128]{1,0:T(8,128)(2,1)} %bias_rest.1, f32[3]{0:T(128)} %convert_element_type.3.bias_out, bf16[3,3,256,128]{3,2,1,0:T(8,128)(2,1)} %w_first.1, ...), custom_call_target="tpu_custom_call" | custom-call | tf_op jit(solution)/shard_map/pallas_call | solution.py:447
  171.0 1.7 copy.11

commit v3 on v2

--- a/solution.py
+++ b/solution.py
@@ -30,10 +30,10 @@
         column_lanes = (planes + 2) * lanes
         flat_width = -(-(ext_w * column_lanes) // 128) * 128
 
-        def kernel(act_hbm, norm_first, norm_rest, bias_rest, bias_out, w_first, w_short, w_rest, w_out, out_ref,
-                   a_ext, t_ext, h_ext, a_ud, t_ud, h_ud, act_a, act_m, wp_first, wp_rest, w_head, reorder, image_rows,
+        def kernel(act_hbm, norm_first, norm_rest, bias_rest, bias_out, w_first_hbm, w_short, w_rest_hbm, w_out, out_ref,
+                   a_ext, t_ext, h_ext, a_ud, t_ud, h_ud, act_a0, act_a1, act_m0, act_m1, w_first, w_rest, wp_first, wp_rest, w_head, reorder, image_rows,
                    raw, stage_lo, stage_hi, rx1, rx2, rx1a, rx2a,
-                   raw_sem, col_send, col_recv, row_send, row_recv, st1_send, st1_recv, st2_send, st2_recv):
+                   raw_sem, weight_sem, col_send, col_recv, row_send, row_recv, st1_send, st1_recv, st2_send, st2_recv):
             my_y = lax.axis_index("sy")
             my_x = lax.axis_index("sx")
             has_up = my_y > 0
@@ -49,7 +49,12 @@
             def fetch(sample, slot):
                 return pltpu.make_async_copy(act_hbm.at[sample], raw.at[slot], raw_sem.at[slot])
 
+            first_in = pltpu.make_async_copy(w_first_hbm, w_first, weight_sem.at[0])
+            rest_in = pltpu.make_async_copy(w_rest_hbm, w_rest, weight_sem.at[1])
             fetch(0, 0).start()
+            first_in.start()
+            rest_in.start()
+            pl.semaphore_wait(barrier, rows_n * cols_n - 1)
 
             def pair_weights(dst, src, chans):
                 for dc in range(3):
@@ -58,23 +63,6 @@
                         zero = jnp.zeros((chans, 128), bf16)
                         dst[pl.ds(base, chans), 0:128] = src(j, dc) if j < 3 else zero
                         dst[pl.ds(base, chans), 128:256] = src(j - 1, dc) if j > 0 else zero
-
-            pair_weights(wp_first, lambda dr, dc: w_first[dr, dc], 256)
-
-            def pair_rest(index, carry):
-                pair_weights(wp_rest.at[index], lambda dr, dc: w_rest[index, dr, dc], 128)
-                return carry
-
-            lax.fori_loop(0, 5, pair_rest, 0)
-
-            for tap in range(9):
-                taps3 = w_out[tap // 3, tap % 3].astype(f32)
-                w_head[pl.ds(8 * tap, 8), :] = jnp.concatenate([taps3, jnp.zeros((5, 128), f32)], axis=0)
-            from_id = lax.broadcasted_iota(jnp.int32, (tile_h, tile_h), 0)
-            to_id = lax.broadcasted_iota(jnp.int32, (tile_h, tile_h), 1)
-            reorder[...] = jnp.where(lax.rem(from_id, lanes) * planes + from_id // lanes == to_id, 1.0, 0.0).astype(bf16)
-
-            pl.semaphore_wait(barrier, rows_n * cols_n - 1)
 
             def span(batch):
                 return pl.ds(batch * BATCH, BATCH)
@@ -237,38 +225,54 @@
                     return result[0]
                 return tuple(jnp.concatenate([result[0][i], result[1][i]], axis=1) for i in range(2))
 
+            half_planes = planes // 2
+
             def activate(layer, sample):
                 ext, ud, _, _, _ = layer_out(layer)
-                dst = act_a if layer == 0 else act_m
+                upper, lower = (act_a0, act_a1) if layer == 0 else (act_m0, act_m1)
                 chans = 256 if layer == 0 else 128
                 scale, shift = scale_shift(layer, sample)
                 scale3 = scale.reshape(1, 1, chans)
                 shift3 = shift.reshape(1, 1, chans)
+                shape = (ext_w, lanes, chans)
+                col_id = lax.broadcasted_iota(jnp.int32, shape, 0)
+                row_id = lax.broadcasted_iota(jnp.int32, shape, 1)
+                in_cols = (col_id >= jnp.where(has_left, 0, 1)) & (col_id <= jnp.where(has_right, ext_w - 1, ext_w - 2))
 
                 def silu(x):
                     half = x.astype(f32) * scale3 + shift3
                     return half + half * jnp.tanh(half)
 
-                for q in range(planes):
-                    dst[(q + 1) // 2, (q + 1) % 2, pl.ds(1, tile_w)] = silu(ext[sample, q, pl.ds(1, tile_w)]).astype(bf16)
-                for col, cond in ((0, has_left), (ext_w - 1, has_right)):
-                    for q in range(planes):
-                        value = silu(ext[sample, q, pl.ds(col, 1)])
-                        dst[(q + 1) // 2, (q + 1) % 2, pl.ds(col, 1)] = jnp.where(cond, value, 0.0).astype(bf16)
-                shape = (ext_w, lanes, chans)
-                col_id = lax.broadcasted_iota(jnp.int32, shape, 0)
-                row_id = lax.broadcasted_iota(jnp.int32, shape, 1)
-                col_lo = jnp.where(has_left, 0, 1)
-                col_hi = jnp.where(has_right, ext_w - 1, ext_w - 2)
-                in_cols = (col_id >= col_lo) & (col_id <= col_hi)
-                for side, cond, near, far, turn, edge in ((0, has_up, planes, 0, 1, 0), (1, has_down, 1, planes + 1, lanes - 1, lanes - 1)):
-                    own = pltpu.roll(dst[near // 2, near % 2].astype(f32), turn, axis=1)
-                    other = pltpu.roll(silu(ud[side, sample]), turn, axis=1)
-                    other = jnp.where(in_cols & cond, other, 0.0)
-                    dst[far // 2, far % 2] = jnp.where(row_id == edge, other, own).astype(bf16)
-
-            def convolve(layer, sample):
-                src = act_a if layer == 1 else act_m
+                def put(plane, cols, value):
+                    if plane <= half_planes + 1:
+                        upper[plane // 2, plane % 2, cols] = value
+                    if plane >= half_planes:
+                        lower[(plane - half_planes) // 2, plane % 2, cols] = value
+
+                def tile_plane(q):
+                    put(q + 1, pl.ds(1, tile_w), silu(ext[sample, q, pl.ds(1, tile_w)]).astype(bf16))
+                    for col, cond in ((0, has_left), (ext_w - 1, has_right)):
+                        put(q + 1, pl.ds(col, 1), jnp.where(cond, silu(ext[sample, q, pl.ds(col, 1)]), 0.0).astype(bf16))
+
+                def border_plane(near, plane, side, cond, turn, edge):
+                    own = pltpu.roll(jnp.where(in_cols, silu(ext[sample, near]), 0.0), turn, axis=1)
+                    other = pltpu.roll(jnp.where(in_cols & cond, silu(ud[side, sample]), 0.0), turn, axis=1)
+                    put(plane, slice(None), jnp.where(row_id == edge, other, own).astype(bf16))
+
+                def fill_upper():
+                    border_plane(planes - 1, 0, 0, has_up, 1, 0)
+                    for q in range(half_planes + 1):
+                        tile_plane(q)
+
+                def fill_lower():
+                    for q in range(half_planes + 1, planes):
+                        tile_plane(q)
+                    border_plane(0, planes + 1, 1, has_down, lanes - 1, lanes - 1)
+
+                return fill_upper, fill_lower
+
+            def activate_convolve(layer, sample):
+                fill_upper, fill_lower = activate(layer - 1, sample)
                 chans = 256 if layer == 1 else 128
                 ext, _, parity, sums_one, _ = layer_out(layer)
                 bias_rows = bias_rest[...].astype(f32)
@@ -276,20 +280,20 @@
                 if layer == 2:
                     bias = bias + bias_rows[6:7]
                 weights = wp_first if layer == 1 else wp_rest.at[layer - 2]
-                sum_one = jnp.zeros((8, 128), f32)
-                sum_two = jnp.zeros((8, 128), f32)
-                parts = 2
-                half = pairs // parts
-                for part in range(parts):
-                    pieces = []
-                    for dc in range(3):
-                        for j in range(4):
-                            piece = src[pl.ds(part * half + j // 2, half), j % 2, pl.ds(dc, tile_w)]
-                            pieces.append(piece.reshape(half * tile_w * lanes, chans))
-                    accum = jnp.dot(jnp.concatenate(pieces, axis=1), weights[...], preferred_element_type=f32)
-                    for k in range(half):
+                sums = [jnp.zeros((8, 128), f32), jnp.zeros((8, 128), f32)]
+                parts = 4
+                share = pairs // parts
+
+                def product(part):
+                    src = ((act_a0, act_a1) if layer == 1 else (act_m0, act_m1))[part // 2]
+                    base = part % 2 * share
+                    pieces = [src[pl.ds(base + j // 2, share), j % 2, pl.ds(dc, tile_w)].reshape(share * tile_w * lanes, chans) for dc in range(3) for j in range(4)]
+                    return jnp.dot(jnp.concatenate(pieces, axis=1), weights[...], preferred_element_type=f32)
+
+                def finish(part, accum):
+                    for k in range(share):
                         for odd in range(2):
-                            q = 2 * (part * half + k) + odd
+                            q = 2 * (part * share + k) + odd
                             value = accum[k * 128:(k + 1) * 128, odd * 128:(odd + 1) * 128].reshape(tile_w, lanes, 128) + bias.reshape(1, 1, 128)
                             if layer == 2:
                                 skip = jnp.dot(a_ext[sample, q, pl.ds(1, tile_w)].reshape(128, 256), w_short[...], preferred_element_type=f32)
@@ -299,25 +303,34 @@
                             value = value.astype(bf16)
                             ext[sample, q, pl.ds(1, tile_w)] = value
                             wide = value.astype(f32).reshape(tile_w * 2, 8, 128)
-                            sum_one = sum_one + jnp.sum(wide, axis=0)
-                            sum_two = sum_two + jnp.sum(wide * wide, axis=0)
+                            sums[0] = sums[0] + jnp.sum(wide, axis=0)
+                            sums[1] = sums[1] + jnp.sum(wide * wide, axis=0)
+
+                fill_upper()
+                first = [product(0), product(1)]
+                fill_lower()
+                for part in range(2):
+                    finish(part, first[part])
+                second = [product(2), product(3)]
+                for part in range(2):
+                    finish(2 + part, second[part])
                 sums_one[parity, sample // BATCH, my_y, lax.rem(sample, BATCH)] = jnp.concatenate(
-                    [jnp.sum(sum_one, axis=0, keepdims=True), jnp.sum(sum_two, axis=0, keepdims=True)], axis=0)
+                    [jnp.sum(sums[0], axis=0, keepdims=True), jnp.sum(sums[1], axis=0, keepdims=True)], axis=0)
 
             def load_step(index, batch):
                 sample = batch * BATCH + index
                 slot = lax.rem(sample, 2)
+
+                @pl.when(sample > 0)
+                def _():
+                    send_columns(0, sample - 1)
+
+                @pl.when(sample + 1 < samples)
+                def _():
+                    fetch(sample + 1, 1 - slot).start()
+
+                within(0, batch, index)
                 fetch(sample, slot).wait()
-
-                @pl.when(sample + 1 < samples)
-                def _():
-                    fetch(sample + 1, 1 - slot).start()
-
-                @pl.when(sample > 0)
-                def _():
-                    send_columns(0, sample - 1)
-
-                within(0, batch, index)
                 for chunk in range(tile_h // 16):
                     piece = raw[slot, pl.ds(chunk * 16, 16)].astype(f32).reshape(16 * tile_w, 256)
                     stage_lo[pl.ds(chunk * 16 * tile_w, 16 * tile_w), :] = piece[:, :128]
@@ -344,6 +357,23 @@
             send_columns(0, samples - 1)
             send_sums(0, batches - 1)
 
+            first_in.wait()
+            rest_in.wait()
+            pair_weights(wp_first, lambda dr, dc: w_first[dr, dc], 256)
+
+            def pair_rest(index, carry):
+                pair_weights(wp_rest.at[index], lambda dr, dc: w_rest[index, dr, dc], 128)
+                return carry
+
+            lax.fori_loop(0, 5, pair_rest, 0)
+
+            for tap in range(9):
+                taps3 = w_out[tap // 3, tap % 3].astype(f32)
+                w_head[pl.ds(8 * tap, 8), :] = jnp.concatenate([taps3, jnp.zeros((5, 128), f32)], axis=0)
+            from_id = lax.broadcasted_iota(jnp.int32, (tile_h, tile_h), 0)
+            to_id = lax.broadcasted_iota(jnp.int32, (tile_h, tile_h), 1)
+            reorder[...] = jnp.where(lax.rem(from_id, lanes) * planes + from_id // lanes == to_id, 1.0, 0.0).astype(bf16)
+
             for layer in range(1, 7):
                 def conv_step(index, batch, layer=layer):
                     sample = batch * BATCH + index
@@ -353,8 +383,7 @@
                         send_columns(layer, sample - 1)
 
                     within(layer, batch, index)
-                    activate(layer - 1, sample)
-                    convolve(layer, sample)
+                    activate_convolve(layer, sample)
                     return batch
 
                 def conv_batch(batch, carry, layer=layer, conv_step=conv_step):
@@ -374,8 +403,11 @@
                 def _():
                     send_totals(6, batches + batch - 2)
 
-                activate(6, sample)
-                flat = jnp.swapaxes(act_m[...].reshape(planes + 2, ext_w, lanes, 128), 0, 1).reshape(ext_w * column_lanes, 128)
+                for fill in activate(6, sample):
+                    fill()
+                rows = half_planes + 2
+                flat = jnp.concatenate([act_m0[...].reshape(rows, ext_w, lanes, 128), act_m1[...].reshape(rows, ext_w, lanes, 128)[2:]], axis=0)
+                flat = jnp.swapaxes(flat, 0, 1).reshape(ext_w * column_lanes, 128)
                 flat = jnp.concatenate([flat, jnp.zeros((flat_width - flat.shape[0], 128), bf16)], axis=0)
                 taps = lax.dot_general(w_head[...].astype(bf16), flat, (((1,), (1,)), ((), ())), preferred_element_type=f32)
                 image = taps[0:8]
@@ -413,6 +445,7 @@
         kernel, lanes, planes, ext_w = make_kernel(samples, tile_h, tile_w)
         batches = samples // BATCH
         vmem = pl.BlockSpec(memory_space=pltpu.VMEM)
+        hbm = pl.BlockSpec(memory_space=pl.ANY)
         scratch = [
             pltpu.VMEM((samples, planes, ext_w, lanes, 256), bf16),
             pltpu.VMEM((samples, planes, ext_w, lanes, 128), bf16),
@@ -420,8 +453,12 @@
             pltpu.VMEM((2, samples, ext_w, lanes, 256), bf16),
             pltpu.VMEM((2, samples, ext_w, lanes, 128), bf16),
             pltpu.VMEM((2, samples, ext_w, lanes, 128), bf16),
-            pltpu.VMEM(((planes + 2) // 2, 2, ext_w, lanes, 256), bf16),
-            pltpu.VMEM(((planes + 2) // 2, 2, ext_w, lanes, 128), bf16),
+            pltpu.VMEM((planes // 4 + 1, 2, ext_w, lanes, 256), bf16),
+            pltpu.VMEM((planes // 4 + 1, 2, ext_w, lanes, 256), bf16),
+            pltpu.VMEM((planes // 4 + 1, 2, ext_w, lanes, 128), bf16),
+            pltpu.VMEM((planes // 4 + 1, 2, ext_w, lanes, 128), bf16),
+            pltpu.VMEM((3, 3, 256, 128), bf16),
+            pltpu.VMEM((5, 3, 3, 128, 128), bf16),
             pltpu.VMEM((12 * 256, 256), bf16),
             pltpu.VMEM((5, 12 * 128, 256), bf16),
             pltpu.VMEM((72, 128), f32),
@@ -435,6 +472,7 @@
             pltpu.VMEM((1, batches, rows_n, BATCH, 4, 128), f32),
             pltpu.VMEM((1, batches, cols_n, BATCH, 1, 128), f32),
             pltpu.SemaphoreType.DMA((2,)),
+            pltpu.SemaphoreType.DMA((2,)),
             pltpu.SemaphoreType.DMA((samples, 2)),
             pltpu.SemaphoreType.DMA((2, samples, 2)),
             pltpu.SemaphoreType.DMA((batches, 2)),
@@ -447,7 +485,7 @@
         image = pl.pallas_call(
             kernel,
             out_shape=jax.ShapeDtypeStruct((samples, 3, tile_w, tile_h), f32),
-            in_specs=[pl.BlockSpec(memory_space=pl.ANY), vmem, vmem, vmem, pl.BlockSpec(memory_space=pltpu.SMEM), vmem, vmem, vmem, vmem],
+            in_specs=[hbm, vmem, vmem, vmem, pl.BlockSpec(memory_space=pltpu.SMEM), hbm, vmem, hbm, vmem],
             out_specs=vmem,
             scratch_shapes=scratch,
             compiler_params=pltpu.CompilerParams(collective_id=0, has_side_effects=True, vmem_limit_bytes=60 * 1024 * 1024),

time: 173 us -> 172 us (level)
  no operation moved by 1% of the time
where the time goes in v3:
time: 172 us
  Pallas kernels  169 us (98%)
    pallas_call x1, Pallas kernels, local_decode(): pl.pallas_call(kernel, out_shape=jax.ShapeDtypeStruct((samples, 3, tile_w...  169 us

profile of v3, /device:TPU:0, one launch (start us, length us, event | category | flops | bytes accessed | tf_op | source)
XLA Modules:
  0.0 171.5 jit_solution(17010591246970780463)
XLA Ops:
  0.0 1.2 convert_element_type.3.bias_out
  1.2 168.6 %shard_map.91 = f32[12,3,8,256]{3,2,1,0:T(8,128)} custom-call(bf16[12,256,8,256]{3,2,1,0:T(8,128)(2,1)} %act_hbm.1, bf16[2,256]{1,0:T(2,128)(2,1)} %norm_first.1, bf16[6,2,128]{2,1,0:T(2,128)(2,1)} %norm_rest.1, bf16[7,128]{1,0:T(8,128)(2,1)} %bias_rest.1, f32[3]{0:T(128)} %convert_element_type.3.bias_out, bf16[3,3,256,128]{3,2,1,0:T(8,128)(2,1)} %w_first_hbm.1, ...), custom_call_target="tpu_custom_call" | custom-call | tf_op jit(solution)/shard_map/pallas_call | solution.py:485
  169.8 1.7 copy.11

commit v4 on v3

--- a/solution.py
+++ b/solution.py
@@ -32,8 +32,8 @@
 
         def kernel(act_hbm, norm_first, norm_rest, bias_rest, bias_out, w_first_hbm, w_short, w_rest_hbm, w_out, out_ref,
                    a_ext, t_ext, h_ext, a_ud, t_ud, h_ud, act_a0, act_a1, act_m0, act_m1, w_first, w_rest, wp_first, wp_rest, w_head, reorder, image_rows,
-                   raw, stage_lo, stage_hi, rx1, rx2, rx1a, rx2a,
-                   raw_sem, weight_sem, col_send, col_recv, row_send, row_recv, st1_send, st1_recv, st2_send, st2_recv):
+                   raw, rx1, rx2, rx1a, rx2a,
+                   raw_sem, weight_sem, first_send, first_recv, col_send, col_recv, row_send, row_recv, st1_send, st1_recv, st2_send, st2_recv):
             my_y = lax.axis_index("sy")
             my_x = lax.axis_index("sx")
             has_up = my_y > 0
@@ -46,12 +46,14 @@
                 other = lax.rem(my_y * cols_n + my_x + step, rows_n * cols_n)
                 pl.semaphore_signal(barrier, inc=1, device_id={"sy": other // cols_n, "sx": lax.rem(other, cols_n)}, device_id_type=MESH)
 
-            def fetch(sample, slot):
-                return pltpu.make_async_copy(act_hbm.at[sample], raw.at[slot], raw_sem.at[slot])
+            def fetch(sample):
+                slot = lax.rem(sample, 2)
+                return [pltpu.make_async_copy(act_hbm.at[sample, pl.ds(4 * part, 4)], raw.at[slot, pl.ds(4 * part, 4)], raw_sem.at[slot, part]) for part in range(lanes // 4)]
 
             first_in = pltpu.make_async_copy(w_first_hbm, w_first, weight_sem.at[0])
             rest_in = pltpu.make_async_copy(w_rest_hbm, w_rest, weight_sem.at[1])
-            fetch(0, 0).start()
+            for copy in fetch(0):
+                copy.start()
             first_in.start()
             rest_in.start()
             pl.semaphore_wait(barrier, rows_n * cols_n - 1)
@@ -71,9 +73,17 @@
                 return pltpu.make_async_remote_copy(src_ref=src, dst_ref=dst, send_sem=send_sem, recv_sem=recv_sem,
                                                     device_id={"sy": to_y, "sx": to_x}, device_id_type=MESH)
 
-            def column_copies(ext, parity, sample):
+            def column_copies(layer, batch):
+                ext, _, parity, _, _ = layer_out(layer)
                 moves = [(has_left, has_right, 1, ext_w - 1, my_x - 1), (has_right, has_left, ext_w - 2, 0, my_x + 1)]
-                return [(leaves, arrives, remote(ext.at[sample, :, src], ext.at[sample, :, dst], col_send.at[sample, index], col_recv.at[parity, sample, index], my_y, to_x))
+                if layer == 0:
+                    return [copy for index in range(BATCH) for copy in first_columns(batch * BATCH + index)]
+                return [(leaves, arrives, remote(ext.at[span(batch), :, src], ext.at[span(batch), :, dst], col_send.at[batch, index], col_recv.at[parity, batch, index], my_y, to_x))
+                        for index, (leaves, arrives, src, dst, to_x) in enumerate(moves)]
+
+            def first_columns(sample):
+                moves = [(has_left, has_right, 1, ext_w - 1, my_x - 1), (has_right, has_left, ext_w - 2, 0, my_x + 1)]
+                return [(leaves, arrives, remote(a_ext.at[sample, :, src], a_ext.at[sample, :, dst], first_send.at[sample, index], first_recv.at[sample, index], my_y, to_x))
                         for index, (leaves, arrives, src, dst, to_x) in enumerate(moves)]
 
             def row_copies(ext, ud, parity, batch):
@@ -103,10 +113,11 @@
                 def _():
                     copy.start()
 
-            def send_columns(layer, sample):
-                ext, _, parity, _, _ = layer_out(layer)
-                for leaves, _, copy in column_copies(ext, parity, sample):
-                    start_if(leaves, copy)
+            def send_batch(layer, batch):
+                if layer > 0:
+                    for leaves, _, copy in column_copies(layer, batch):
+                        start_if(leaves, copy)
+                send_sums(layer, batch)
 
             def send_sums(layer, batch):
                 _, _, parity, sums_one, _ = layer_out(layer)
@@ -115,11 +126,10 @@
 
             def pass_on(layer, batch):
                 ext, ud, parity, sums_one, sums_two = layer_out(layer)
-                for index in range(BATCH):
-                    for _, arrives, copy in column_copies(ext, parity, batch * BATCH + index):
-                        @pl.when(arrives)
-                        def _(copy=copy):
-                            copy.wait_recv()
+                for _, arrives, copy in column_copies(layer, batch):
+                    @pl.when(arrives)
+                    def _(copy=copy):
+                        copy.wait_recv()
                 for leaves, _, copy in row_copies(ext, ud, parity, batch):
                     start_if(leaves, copy)
                 for copy in peers(sums_one, st1_send, st1_recv, parity, batch, True):
@@ -137,28 +147,29 @@
                     copy.start()
 
             def boundary(layer, batch):
-                @pl.when(batch > 0)
-                def _():
-                    send_sums(layer, batch - 1)
-
-                @pl.when(batch >= 2)
-                def _():
-                    pass_on(layer, batch - 2)
+                if layer < 7:
+                    @pl.when(batch > 0)
+                    def _():
+                        send_batch(layer, batch - 1)
+
+                    @pl.when(batch >= 3)
+                    def _():
+                        send_totals(layer, batch - 3)
+
+                if layer > 0:
+                    @pl.when(batch < 3)
+                    def _():
+                        send_totals(layer - 1, batches + batch - 3)
+
+                if layer < 7:
+                    @pl.when(batch >= 2)
+                    def _():
+                        pass_on(layer, batch - 2)
 
                 if layer > 0:
                     @pl.when(batch < 2)
                     def _():
                         pass_on(layer - 1, batches + batch - 2)
-
-            def within(layer, batch, index):
-                @pl.when((index == 1) & (batch >= 2))
-                def _():
-                    send_totals(layer, batch - 2)
-
-                if layer > 0:
-                    @pl.when((index == 1) & (batch < 2))
-                    def _():
-                        send_totals(layer - 1, batches + batch - 2)
 
             def await_batch(layer, batch):
                 ext, ud, parity, sums_one, sums_two = layer_out(layer)
@@ -171,11 +182,10 @@
                     @pl.when(leaves)
                     def _(copy=copy):
                         copy.wait_send()
-                for index in range(BATCH):
-                    for leaves, _, copy in column_copies(ext, parity, batch * BATCH + index):
-                        @pl.when(leaves)
-                        def _(copy=copy):
-                            copy.wait_send()
+                for leaves, _, copy in column_copies(layer, batch):
+                    @pl.when(leaves)
+                    def _(copy=copy):
+                        copy.wait_send()
                 for copy in peers(sums_one, st1_send, st1_recv, parity, batch, True):
                     copy.wait_send()
                 for copy in peers(sums_two, st2_send, st2_recv, parity, batch, False):
@@ -319,33 +329,31 @@
 
             def load_step(index, batch):
                 sample = batch * BATCH + index
-                slot = lax.rem(sample, 2)
 
                 @pl.when(sample > 0)
                 def _():
-                    send_columns(0, sample - 1)
+                    for leaves, _, copy in first_columns(sample - 1):
+                        start_if(leaves, copy)
 
                 @pl.when(sample + 1 < samples)
                 def _():
-                    fetch(sample + 1, 1 - slot).start()
-
-                within(0, batch, index)
-                fetch(sample, slot).wait()
-                for chunk in range(tile_h // 16):
-                    piece = raw[slot, pl.ds(chunk * 16, 16)].astype(f32).reshape(16 * tile_w, 256)
-                    stage_lo[pl.ds(chunk * 16 * tile_w, 16 * tile_w), :] = piece[:, :128]
-                    stage_hi[pl.ds(chunk * 16 * tile_w, 16 * tile_w), :] = piece[:, 128:]
-                for half, stage in ((0, stage_lo), (1, stage_hi)):
-                    sum_one = jnp.zeros((lanes, 128), f32)
-                    sum_two = jnp.zeros((lanes, 128), f32)
-                    for q in range(planes):
-                        for c in range(tile_w):
-                            value = stage[pl.ds(q * tile_w + c, lanes, stride=planes * tile_w), :]
-                            a_ext[sample, q, c + 1, :, half * 128:(half + 1) * 128] = value.astype(bf16)
-                            sum_one = sum_one + value
-                            sum_two = sum_two + value * value
-                    rx1a[0, sample // BATCH, my_y, lax.rem(sample, BATCH), half:half + 1] = jnp.sum(sum_one, axis=0, keepdims=True)
-                    rx1a[0, sample // BATCH, my_y, lax.rem(sample, BATCH), half + 2:half + 3] = jnp.sum(sum_two, axis=0, keepdims=True)
+                    for copy in fetch(sample + 1):
+                        copy.start()
+
+                for copy in fetch(sample):
+                    copy.wait()
+                slot = lax.rem(sample, 2)
+                sum_one = jnp.zeros((8, 256), f32)
+                sum_two = jnp.zeros((8, 256), f32)
+                for q in range(planes):
+                    value = jnp.swapaxes(raw[slot, :, q].astype(f32), 0, 1)
+                    a_ext[sample, q, pl.ds(1, tile_w)] = value.astype(bf16)
+                    wide = value.reshape(2 * tile_w, 8, 256)
+                    sum_one = sum_one + jnp.sum(wide, axis=0)
+                    sum_two = sum_two + jnp.sum(wide * wide, axis=0)
+                one = jnp.sum(sum_one, axis=0, keepdims=True)
+                two = jnp.sum(sum_two, axis=0, keepdims=True)
+                rx1a[0, batch, my_y, index] = jnp.concatenate([one[:, :128], one[:, 128:], two[:, :128], two[:, 128:]], axis=0)
                 return batch
 
             def load_batch(batch, carry):
@@ -354,8 +362,9 @@
                 return carry
 
             lax.fori_loop(0, batches, load_batch, 0)
-            send_columns(0, samples - 1)
-            send_sums(0, batches - 1)
+            for leaves, _, copy in first_columns(samples - 1):
+                start_if(leaves, copy)
+            send_batch(0, batches - 1)
 
             first_in.wait()
             rest_in.wait()
@@ -376,14 +385,7 @@
 
             for layer in range(1, 7):
                 def conv_step(index, batch, layer=layer):
-                    sample = batch * BATCH + index
-
-                    @pl.when(sample > 0)
-                    def _():
-                        send_columns(layer, sample - 1)
-
-                    within(layer, batch, index)
-                    activate_convolve(layer, sample)
+                    activate_convolve(layer, batch * BATCH + index)
                     return batch
 
                 def conv_batch(batch, carry, layer=layer, conv_step=conv_step):
@@ -393,15 +395,10 @@
                     return carry
 
                 lax.fori_loop(0, batches, conv_batch, 0)
-                send_columns(layer, samples - 1)
-                send_sums(layer, batches - 1)
+                send_batch(layer, batches - 1)
 
             def head_step(index, batch):
                 sample = batch * BATCH + index
-
-                @pl.when((index == 1) & (batch < 2))
-                def _():
-                    send_totals(6, batches + batch - 2)
 
                 for fill in activate(6, sample):
                     fill()
@@ -428,10 +425,7 @@
                 return batch
 
             def head_batch(batch, carry):
-                @pl.when(batch < 2)
-                def _():
-                    pass_on(6, batches + batch - 2)
-
+                boundary(7, batch)
                 await_batch(6, batch)
                 lax.fori_loop(0, BATCH, head_step, batch)
                 return carry
@@ -464,17 +458,17 @@
             pltpu.VMEM((72, 128), f32),
             pltpu.VMEM((tile_h, tile_h), bf16),
             pltpu.VMEM((tile_h // 128, 8 * tile_w, 128), f32),
-            pltpu.VMEM((2, tile_h, tile_w, 256), bf16),
-            pltpu.VMEM((tile_h * tile_w, 128), f32),
-            pltpu.VMEM((tile_h * tile_w, 128), f32),
+            pltpu.VMEM((2, lanes, planes, tile_w, 256), bf16),
             pltpu.VMEM((2, batches, rows_n, BATCH, 2, 128), f32),
             pltpu.VMEM((2, batches, cols_n, BATCH, 1, 128), f32),
             pltpu.VMEM((1, batches, rows_n, BATCH, 4, 128), f32),
             pltpu.VMEM((1, batches, cols_n, BATCH, 1, 128), f32),
-            pltpu.SemaphoreType.DMA((2,)),
+            pltpu.SemaphoreType.DMA((2, lanes // 4)),
             pltpu.SemaphoreType.DMA((2,)),
             pltpu.SemaphoreType.DMA((samples, 2)),
-            pltpu.SemaphoreType.DMA((2, samples, 2)),
+            pltpu.SemaphoreType.DMA((samples, 2)),
+            pltpu.SemaphoreType.DMA((batches, 2)),
+            pltpu.SemaphoreType.DMA((2, batches, 2)),
             pltpu.SemaphoreType.DMA((batches, 2)),
             pltpu.SemaphoreType.DMA((2, batches, 2)),
             pltpu.SemaphoreType.DMA((batches, rows_n)),
@@ -489,7 +483,7 @@
             out_specs=vmem,
             scratch_shapes=scratch,
             compiler_params=pltpu.CompilerParams(collective_id=0, has_side_effects=True, vmem_limit_bytes=60 * 1024 * 1024),
-        )(act_in, norm_first, norm_rest, bias_rest, bias_out.astype(f32), w_first, w_short, w_rest, w_out.transpose(0, 1, 3, 2))
+        )(act_in.reshape(samples, lanes, planes, tile_w, 256), norm_first, norm_rest, bias_rest, bias_out.astype(f32), w_first, w_short, w_rest, w_out.transpose(0, 1, 3, 2))
         return image.transpose(0, 3, 2, 1)
 
     return jax.shard_map(local_decode, mesh=mesh, in_specs=(tile_spec, replicated, replicated, replicated, replicated, replicated, replicated, replicated, replicated), out_specs=tile_spec, check_vma=False)

time: 172 us -> 192 us (1.12)
  Pallas kernels: 169 us -> 189 us
    pallas_call x1, Pallas kernels: 169 us -> 189 us  [local_decode(): pl.pallas_call(kernel, out_shape=jax.ShapeDtypeStruct((samples, 3, tile_w...]
where the time goes in v4:
time: 192 us
  Pallas kernels  189 us (98%)
    pallas_call x1, Pallas kernels, local_decode(): pl.pallas_call(kernel, out_shape=jax.ShapeDtypeStruct((samples, 3, tile_w...  189 us

profile of v4, /device:TPU:0, one launch (start us, length us, event | category | flops | bytes accessed | tf_op | source)
XLA Modules:
  0.0 191.9 jit_solution(15754212111016825680)
XLA Ops:
  0.0 1.2 convert_element_type.3.bias_out
  1.2 189.0 %shard_map.91 = f32[12,3,8,256]{3,2,1,0:T(8,128)} custom-call(bf16[12,16,16,8,256]{4,3,2,1,0:T(8,128)(2,1)} %bitcast.3, bf16[2,256]{1,0:T(2,128)(2,1)} %norm_first.1, bf16[6,2,128]{2,1,0:T(2,128)(2,1)} %norm_rest.1, bf16[7,128]{1,0:T(8,128)(2,1)} %bias_rest.1, f32[3]{0:T(128)} %convert_element_type.3.bias_out, bf16[3,3,256,128]{3,2,1,0:T(8,128)(2,1)} %w_first_hbm.1, ...), custom_call_target="tpu_custom_call" | custom-call | tf_op jit(solution)/shard_map/pallas_call | solution.py:479
  190.2 1.7 copy.11

commit v5 on v4

--- a/solution.py
+++ b/solution.py
@@ -33,7 +33,7 @@
         def kernel(act_hbm, norm_first, norm_rest, bias_rest, bias_out, w_first_hbm, w_short, w_rest_hbm, w_out, out_ref,
                    a_ext, t_ext, h_ext, a_ud, t_ud, h_ud, act_a0, act_a1, act_m0, act_m1, w_first, w_rest, wp_first, wp_rest, w_head, reorder, image_rows,
                    raw, rx1, rx2, rx1a, rx2a,
-                   raw_sem, weight_sem, first_send, first_recv, col_send, col_recv, row_send, row_recv, st1_send, st1_recv, st2_send, st2_recv):
+                   raw_sem, weight_sem, col_send, col_recv, row_send, row_recv, st1_send, st1_recv, st2_send, st2_recv):
             my_y = lax.axis_index("sy")
             my_x = lax.axis_index("sx")
             has_up = my_y > 0
@@ -73,18 +73,14 @@
                 return pltpu.make_async_remote_copy(src_ref=src, dst_ref=dst, send_sem=send_sem, recv_sem=recv_sem,
                                                     device_id={"sy": to_y, "sx": to_x}, device_id_type=MESH)
 
-            def column_copies(layer, batch):
+            def sample_columns(layer, sample):
                 ext, _, parity, _, _ = layer_out(layer)
                 moves = [(has_left, has_right, 1, ext_w - 1, my_x - 1), (has_right, has_left, ext_w - 2, 0, my_x + 1)]
-                if layer == 0:
-                    return [copy for index in range(BATCH) for copy in first_columns(batch * BATCH + index)]
-                return [(leaves, arrives, remote(ext.at[span(batch), :, src], ext.at[span(batch), :, dst], col_send.at[batch, index], col_recv.at[parity, batch, index], my_y, to_x))
+                return [(leaves, arrives, remote(ext.at[sample, :, src], ext.at[sample, :, dst], col_send.at[sample, index], col_recv.at[parity, sample, index], my_y, to_x))
                         for index, (leaves, arrives, src, dst, to_x) in enumerate(moves)]
 
-            def first_columns(sample):
-                moves = [(has_left, has_right, 1, ext_w - 1, my_x - 1), (has_right, has_left, ext_w - 2, 0, my_x + 1)]
-                return [(leaves, arrives, remote(a_ext.at[sample, :, src], a_ext.at[sample, :, dst], first_send.at[sample, index], first_recv.at[sample, index], my_y, to_x))
-                        for index, (leaves, arrives, src, dst, to_x) in enumerate(moves)]
+            def column_copies(layer, batch):
+                return [copy for index in range(BATCH) for copy in sample_columns(layer, batch * BATCH + index)]
 
             def row_copies(ext, ud, parity, batch):
                 moves = [(has_up, has_down, 0, 1, my_y - 1), (has_down, has_up, planes - 1, 0, my_y + 1)]
@@ -124,14 +120,17 @@
                 for copy in peers(sums_one, st1_send, st1_recv, parity, batch, True):
                     copy.start()
 
-            def pass_on(layer, batch):
-                ext, ud, parity, sums_one, sums_two = layer_out(layer)
+            def relay_rows(layer, batch):
+                ext, ud, parity, _, _ = layer_out(layer)
                 for _, arrives, copy in column_copies(layer, batch):
                     @pl.when(arrives)
                     def _(copy=copy):
                         copy.wait_recv()
                 for leaves, _, copy in row_copies(ext, ud, parity, batch):
                     start_if(leaves, copy)
+
+            def fold_sums(layer, batch):
+                _, _, parity, sums_one, sums_two = layer_out(layer)
                 for copy in peers(sums_one, st1_send, st1_recv, parity, batch, True):
                     copy.wait_recv()
                 total = sums_one[parity, batch, 0]
@@ -155,21 +154,23 @@
                     @pl.when(batch >= 3)
                     def _():
                         send_totals(layer, batch - 3)
+                        relay_rows(layer, batch - 3)
 
                 if layer > 0:
                     @pl.when(batch < 3)
                     def _():
                         send_totals(layer - 1, batches + batch - 3)
+                        relay_rows(layer - 1, batches + batch - 3)
 
                 if layer < 7:
                     @pl.when(batch >= 2)
                     def _():
-                        pass_on(layer, batch - 2)
+                        fold_sums(layer, batch - 2)
 
                 if layer > 0:
                     @pl.when(batch < 2)
                     def _():
-                        pass_on(layer - 1, batches + batch - 2)
+                        fold_sums(layer - 1, batches + batch - 2)
 
             def await_batch(layer, batch):
                 ext, ud, parity, sums_one, sums_two = layer_out(layer)
@@ -332,7 +333,7 @@
 
                 @pl.when(sample > 0)
                 def _():
-                    for leaves, _, copy in first_columns(sample - 1):
+                    for leaves, _, copy in sample_columns(0, sample - 1):
                         start_if(leaves, copy)
 
                 @pl.when(sample + 1 < samples)
@@ -362,7 +363,7 @@
                 return carry
 
             lax.fori_loop(0, batches, load_batch, 0)
-            for leaves, _, copy in first_columns(samples - 1):
+            for leaves, _, copy in sample_columns(0, samples - 1):
                 start_if(leaves, copy)
             send_batch(0, batches - 1)
 
@@ -466,9 +467,7 @@
             pltpu.SemaphoreType.DMA((2, lanes // 4)),
             pltpu.SemaphoreType.DMA((2,)),
             pltpu.SemaphoreType.DMA((samples, 2)),
-            pltpu.SemaphoreType.DMA((samples, 2)),
-            pltpu.SemaphoreType.DMA((batches, 2)),
-            pltpu.SemaphoreType.DMA((2, batches, 2)),
+            pltpu.SemaphoreType.DMA((2, samples, 2)),
             pltpu.SemaphoreType.DMA((batches, 2)),
             pltpu.SemaphoreType.DMA((2, batches, 2)),
             pltpu.SemaphoreType.DMA((batches, rows_n)),

time: 192 us -> 194 us (1.010)
  Pallas kernels: 189 us -> 191 us
where the time goes in v5:
time: 194 us; the launch traced here: 193 us
  Pallas kernels  191 us (98%)
    pallas_call x1, Pallas kernels, local_decode(): pl.pallas_call(kernel, out_shape=jax.ShapeDtypeStruct((samples, 3, tile_w...  191 us

profile of v5, /device:TPU:0, one launch (start us, length us, event | category | flops | bytes accessed | tf_op | source)
XLA Modules:
  0.0 193.4 jit_solution(3587780532458837406)
XLA Ops:
  0.0 1.2 convert_element_type.3.bias_out
  1.2 190.5 %shard_map.91 = f32[12,3,8,256]{3,2,1,0:T(8,128)} custom-call(bf16[12,16,16,8,256]{4,3,2,1,0:T(8,128)(2,1)} %bitcast.3, bf16[2,256]{1,0:T(2,128)(2,1)} %norm_first.1, bf16[6,2,128]{2,1,0:T(2,128)(2,1)} %norm_rest.1, bf16[7,128]{1,0:T(8,128)(2,1)} %bias_rest.1, f32[3]{0:T(128)} %convert_element_type.3.bias_out, bf16[3,3,256,128]{3,2,1,0:T(8,128)(2,1)} %w_first_hbm.1, ...), custom_call_target="tpu_custom_call" | custom-call | tf_op jit(solution)/shard_map/pallas_call | solution.py:478
  191.7 1.7 copy.11

commit v6 on v5

--- a/solution.py
+++ b/solution.py
@@ -147,30 +147,35 @@
 
             def boundary(layer, batch):
                 if layer < 7:
-                    @pl.when(batch > 0)
-                    def _():
-                        send_batch(layer, batch - 1)
+                    @pl.when(batch >= 2)
+                    def _():
+                        fold_sums(layer, batch - 2)
 
                     @pl.when(batch >= 3)
                     def _():
-                        send_totals(layer, batch - 3)
                         relay_rows(layer, batch - 3)
 
                 if layer > 0:
+                    @pl.when(batch < 2)
+                    def _():
+                        fold_sums(layer - 1, batches + batch - 2)
+
                     @pl.when(batch < 3)
                     def _():
-                        send_totals(layer - 1, batches + batch - 3)
                         relay_rows(layer - 1, batches + batch - 3)
+
+                    @pl.when(batch < 2)
+                    def _():
+                        send_totals(layer - 1, batches + batch - 2)
 
                 if layer < 7:
                     @pl.when(batch >= 2)
                     def _():
-                        fold_sums(layer, batch - 2)
-
-                if layer > 0:
-                    @pl.when(batch < 2)
-                    def _():
-                        fold_sums(layer - 1, batches + batch - 2)
+                        send_totals(layer, batch - 2)
+
+                    @pl.when(batch > 0)
+                    def _():
+                        send_batch(layer, batch - 1)
 
             def await_batch(layer, batch):
                 ext, ud, parity, sums_one, sums_two = layer_out(layer)

time: 194 us -> 164 us (0.85)
  Pallas kernels: 191 us -> 161 us
    pallas_call x1, Pallas kernels: 191 us -> 161 us  [local_decode(): pl.pallas_call(kernel, out_shape=jax.ShapeDtypeStruct((samples, 3, tile_w...]
where the time goes in v6:
time: 164 us
  Pallas kernels  161 us (98%)
  local copies, waits for them, and re-layouts  1.69 us (1%)
    pallas_call x1, Pallas kernels, local_decode(): pl.pallas_call(kernel, out_shape=jax.ShapeDtypeStruct((samples, 3, tile_w...  161 us

profile of v6, /device:TPU:0, one launch (start us, length us, event | category | flops | bytes accessed | tf_op | source)
XLA Modules:
  0.0 164.0 jit_solution(9258579947138387293)
XLA Ops:
  0.0 1.2 convert_element_type.3.bias_out
  1.2 161.2 %shard_map.91 = f32[12,3,8,256]{3,2,1,0:T(8,128)} custom-call(bf16[12,16,16,8,256]{4,3,2,1,0:T(8,128)(2,1)} %bitcast.3, bf16[2,256]{1,0:T(2,128)(2,1)} %norm_first.1, bf16[6,2,128]{2,1,0:T(2,128)(2,1)} %norm_rest.1, bf16[7,128]{1,0:T(8,128)(2,1)} %bias_rest.1, f32[3]{0:T(128)} %convert_element_type.3.bias_out, bf16[3,3,256,128]{3,2,1,0:T(8,128)(2,1)} %w_first_hbm.1, ...), custom_call_target="tpu_custom_call" | custom-call | tf_op jit(solution)/shard_map/pallas_call | solution.py:483
  162.3 1.7 %copy.11 = f32[12,256,8,3]{1,2,3,0:T(8,128)} copy(f32[12,256,8,3]{1,2,3,0:T(8,128)} %bitcast.4) | data formatting | bytes 589824

commit v7 on v6

--- a/solution.py
+++ b/solution.py
@@ -167,6 +167,10 @@
                     @pl.when(batch < 2)
                     def _():
                         send_totals(layer - 1, batches + batch - 2)
+
+                    @pl.when(batch == 0)
+                    def _():
+                        send_batch(layer - 1, batches - 1)
 
                 if layer < 7:
                     @pl.when(batch >= 2)
@@ -370,7 +374,6 @@
             lax.fori_loop(0, batches, load_batch, 0)
             for leaves, _, copy in sample_columns(0, samples - 1):
                 start_if(leaves, copy)
-            send_batch(0, batches - 1)
 
             first_in.wait()
             rest_in.wait()
@@ -401,7 +404,6 @@
                     return carry
 
                 lax.fori_loop(0, batches, conv_batch, 0)
-                send_batch(layer, batches - 1)
 
             def head_step(index, batch):
                 sample = batch * BATCH + index

time: 164 us -> 163 us (level)
  no operation moved by 1% of the time
where the time goes in v7:
time: 163 us
  Pallas kernels  160 us (98%)
  local copies, waits for them, and re-layouts  1.69 us (1%)
    pallas_call x1, Pallas kernels, local_decode(): pl.pallas_call(kernel, out_shape=jax.ShapeDtypeStruct((samples, 3, tile_w...  160 us

profile of v7, /device:TPU:0, one launch (start us, length us, event | category | flops | bytes accessed | tf_op | source)
XLA Modules:
  0.0 162.7 jit_solution(9031383590203238535)
XLA Ops:
  0.0 1.2 convert_element_type.3.bias_out
  1.2 159.8 %shard_map.91 = f32[12,3,8,256]{3,2,1,0:T(8,128)} custom-call(bf16[12,16,16,8,256]{4,3,2,1,0:T(8,128)(2,1)} %bitcast.3, bf16[2,256]{1,0:T(2,128)(2,1)} %norm_first.1, bf16[6,2,128]{2,1,0:T(2,128)(2,1)} %norm_rest.1, bf16[7,128]{1,0:T(8,128)(2,1)} %bias_rest.1, f32[3]{0:T(128)} %convert_element_type.3.bias_out, bf16[3,3,256,128]{3,2,1,0:T(8,128)(2,1)} %w_first_hbm.1, ...), custom_call_target="tpu_custom_call" | custom-call | tf_op jit(solution)/shard_map/pallas_call | solution.py:485
  161.0 1.7 %copy.11 = f32[12,256,8,3]{1,2,3,0:T(8,128)} copy(f32[12,256,8,3]{1,2,3,0:T(8,128)} %bitcast.4) | data formatting | bytes 589824
